TPU v7x, 32 devices: a whole 2x2x4 slice. The times are simulated.
32 devices in a mesh: swath: 8 (over y, x, core), chan: 4 (over z).
Axes of the slice: x: 2, y: 2, z: 4, core: 2. Of those that a mesh axis runs over, the one named last changes fastest.
Arguments:
- innovations: float32 [524288], P(('swath', 'chan')), may hold values from -6 to 6
- obs_precision: float32 [524288], P(('swath', 'chan')), may hold values from 0.25 to 4
- jacobian: bfloat16 [524288, 128], P(('swath', 'chan')), may hold values from -0.5 to 0.5
- predictors: float32 [8, 524288], P(None, ('swath', 'chan')), may hold values from -5 to 5
- obs_column: int32 [524288], P(('swath', 'chan')), may hold values from 0 to 2047, as said below
- obs_channel: int32 [524288], P(('swath', 'chan')), may hold values from 0 to 5119
- obs_count: int32 [8, 4], P('swath', 'chan'), may hold values from 5461 to 16384, as said below
- smoothing: float32 [128], replicated, may hold values from 0.02 to 0.12
- bias_precision: float32 [8, 5120], P(None, 'chan'), may hold values from 1 to 100
Outputs:
- control_state: float32 [256, 256, 128], P('swath', 'chan')
- bias_increment: float32 [8, 5120], P(None, 'chan')
- residual_norms: float32 [3], replicated
Inputs may be any that keep to these rules, and one draw needn't show every extreme that they name: `obs_column`: Row-major index latitude row * 64 + longitude column within the tile of the device that holds the slot; all slots of an aligned block of 128 slots lie in one latitude row. `obs_channel`: channel c belongs to block c // 256, whose coefficients are owned by chan index c // 1280. `obs_count`: slots below the count hold live observations, the rest are ignored; some device is full in every draw.
All inputs are finite; a program needn't handle non-finite values.
Results may differ from a plain program's by a relative error of at most 0.0003.
Values sent between devices are 32-bit elements; how exact they have to be, the bound alone decides.
A program may use at most 128 MiB of HBM per device.

v0:
```python
import functools

import jax
import jax.numpy as jnp
from jax import lax
from jax.experimental import pallas as pl
from jax.experimental.pallas import tpu as pltpu
from jax.sharding import PartitionSpec as P

LEV = 128
NPRED = 8
CH_BLOCK = 256
OBS_BLOCK = 128
LAT_DEV = 32
LON_DEV = 64
ITERS = 2
LINES = 8
LANES = 128
F32 = jnp.float32
BF16 = jnp.bfloat16
NT = (((1,), (1,)), ((), ()))
VMEM_LIMIT = 24 * 1024 * 1024


def halves(value):
    high = value.astype(BF16)
    return high, (value - high.astype(F32)).astype(BF16)


def local_kernel(init, blocks, rows_ref, count_ref, cell_ref, chan_ref, prec_ref, pred_ref, jac_ref, *refs):
    if init:
        innov_ref, field_ref, cols_ref, table_ref, acc_ref = refs
    else:
        u_ref, coef_ref, field_ref, cols_ref, table_ref, acc_ref, split_ref, flat_ref = refs
    n_lines = cell_ref.shape[0]
    rows_tab = NPRED * blocks
    tables = 2 if init else 1
    count = count_ref[0, 0]
    field_ref[...] = jnp.zeros_like(field_ref)
    acc_ref[...] = jnp.zeros_like(acc_ref)

    if not init:
        def split_row(i, carry):
            high, low = halves(u_ref[i])
            split_ref[i] = jnp.concatenate([high, low], axis=1)
            return carry

        lax.fori_loop(0, LAT_DEV, split_row, 0)
        for b in range(blocks):
            for h in range(CH_BLOCK // LANES):
                block = coef_ref[b * (CH_BLOCK // LANES) + h]
                flat_ref[b * NPRED : (b + 1) * NPRED, h * LANES : (h + 1) * LANES] = block
        high, low = halves(flat_ref[...])
        coef2 = jnp.concatenate([high, low], axis=1)

    iota_col = lax.broadcasted_iota(jnp.int32, (LON_DEV, OBS_BLOCK), 0)
    iota_ch = lax.broadcasted_iota(jnp.int32, (CH_BLOCK, OBS_BLOCK), 0)
    iota_obs = lax.broadcasted_iota(jnp.int32, (1, OBS_BLOCK), 1)

    def step(it, carry):
        base = pl.multiple_of(it * LINES, LINES)
        cells = cell_ref[pl.ds(base, LINES), :]
        chans = chan_ref[pl.ds(base, LINES), :]
        precs = prec_ref[pl.ds(base, LINES), :]
        if init:
            innovs = innov_ref[pl.ds(base, LINES), :]
        hots, his, masks, weights, preds, jacs, rows = [], [], [], [], [], [], []
        for l in range(LINES):
            ch = chans[l : l + 1, :]
            hots.append(jnp.where(iota_ch == ch % CH_BLOCK, 1.0, 0.0).astype(BF16))
            his.append(jnp.broadcast_to(ch // CH_BLOCK, (NPRED, OBS_BLOCK)))
            masks.append(iota_col == cells[l : l + 1, :] % LON_DEV)
            slot = (base + l) * OBS_BLOCK + iota_obs
            weights.append(jnp.where(slot < count, precs[l : l + 1, :], 0.0))
            start = pl.multiple_of((base + l) * OBS_BLOCK, OBS_BLOCK)
            preds.append(pred_ref[:, pl.ds(start, OBS_BLOCK)])
            jacs.append(jac_ref[pl.ds(start, OBS_BLOCK), :])
            rows.append(rows_ref[base + l])
        values = []
        if init:
            for l in range(LINES):
                values.append(weights[l] * innovs[l : l + 1, :])
        else:
            looked = []
            for l in range(0, LINES, 2):
                pair = jnp.concatenate(hots[l : l + 2], axis=1)
                mid = jnp.dot(
                    coef2, jnp.concatenate([pair, pair], axis=0), preferred_element_type=F32
                )
                for j in range(2):
                    total = jnp.zeros((NPRED, OBS_BLOCK), F32)
                    lanes = slice(j * OBS_BLOCK, (j + 1) * OBS_BLOCK)
                    for b in range(blocks):
                        top = mid[b * NPRED : (b + 1) * NPRED, lanes]
                        total = total + jnp.where(his[l + j] == b, top, 0.0)
                    looked.append(jnp.sum(total * preds[l + j], axis=0, keepdims=True))
            for l in range(LINES):
                twice = jnp.concatenate([jacs[l], jacs[l]], axis=1)
                both = lax.dot_general(split_ref[rows[l]], twice, NT, preferred_element_type=F32)
                seen = jnp.sum(jnp.where(masks[l], both, 0.0), axis=0, keepdims=True)
                values.append(weights[l] * (seen + looked[l]))
        outs = []
        for l in range(LINES):
            high, low = halves(jnp.where(masks[l], values[l], 0.0))
            spread = jnp.concatenate([high, low], axis=1)
            twice = jnp.concatenate([jacs[l], jacs[l]], axis=0)
            outs.append(jnp.dot(spread, twice, preferred_element_type=F32))
        for l in range(LINES):
            field_ref[rows[l]] += outs[l]
        lefts, rights = [], []
        for l in range(LINES):
            highs, lows = [], []
            terms = [preds[l] * values[l]]
            if init:
                terms.append(preds[l] * preds[l] * weights[l])
            for term in terms:
                wide = jnp.concatenate(
                    [jnp.where(his[l] == b, term, 0.0) for b in range(blocks)], axis=0
                )
                high, low = halves(wide)
                highs.append(high)
                lows.append(low)
            lefts.append(jnp.concatenate(highs, axis=0))
            rights.append(jnp.concatenate(lows, axis=0))
        left = jnp.concatenate(lefts + rights, axis=1)
        hot = jnp.concatenate(hots + hots, axis=1)
        acc_ref[...] += lax.dot_general(left, hot, NT, preferred_element_type=F32)
        return carry

    lax.fori_loop(0, n_lines // LINES, step, 0)
    per = CH_BLOCK // LANES
    used = tables * blocks * per
    for t in range(tables):
        for b in range(blocks):
            for h in range(per):
                top = t * rows_tab + b * NPRED
                lanes = slice(h * LANES, (h + 1) * LANES)
                table_ref[(t * blocks + b) * per + h] = acc_ref[top : top + NPRED, lanes]
    if table_ref.shape[0] > used:
        table_ref[used:] = jnp.zeros((table_ref.shape[0] - used, NPRED, LANES), F32)

    def column(i, carry):
        cols_ref[0, pl.ds(i, 1), :] = field_ref[i, 0:1, :]
        cols_ref[1, pl.ds(i, 1), :] = field_ref[i, LON_DEV - 1 : LON_DEV, :]
        return carry

    lax.fori_loop(0, LAT_DEV, column, 0)


def fold(value):
    total = value[0:8]
    for i in range(1, value.shape[0] // 8):
        total = total + value[8 * i : 8 * i + 8]
    return total


def comm_kernel(n, m, width, mode, turn, *refs):
    refs = list(refs)
    take = lambda k: [refs.pop(0) for _ in range(k)]
    smooth_ref, g_ref, gc_ref, table_ref = take(4)
    if mode == "first":
        own_ref, = take(1)
        r_out, rc_ref, u_out, rb_out, diag_out, bp_out, pb_out, scal_out = take(8)
    else:
        p_ref, r_ref, pb_ref, rb_ref, diag_ref, bp_ref, scal_ref = take(7)
        if mode == "middle":
            u_ref, = take(1)
            r_out, rc_ref, p_out, u_out, rb_out, pb_out, scal_out, x_out = take(8)
        else:
            xb_ref, = take(1)
            scal_out, norms_out, bias_out = take(3)
    ta, tf, bb, s1, sc, hu, hd, hc = take(8)
    ta_s, ta_r, h_s, h_r, s1_s, s1_r, b_s, b_r, c_s, c_r, sc_s, sc_r = take(12)
    if mode == "first":
        own_all, o_s, o_r = take(3)
    if mode != "first":
        q_ref, s2, s3, s2_s, s2_r, s3_s, s3_r = take(7)
    if mode != "last":
        hu2, hd2, hc2, k_s, k_r = take(5)
    me = lax.axis_index("swath")
    z = lax.axis_index("chan")
    chunk = table_ref.shape[1]

    def to_lat(d):
        return {"swath": lax.rem(me + d, n)}

    def to_lon(d):
        return {"chan": lax.rem(z + d, m)}

    def send(src, dst, ss, rs, dev):
        copy = pltpu.make_async_remote_copy(
            src_ref=src, dst_ref=dst, send_sem=ss, recv_sem=rs,
            device_id=dev, device_id_type=pl.DeviceIdType.MESH,
        )
        copy.start()
        return copy

    barrier = pltpu.get_barrier_semaphore()
    for d in range(1, n):
        pl.semaphore_signal(barrier, inc=1, device_id=to_lat(d), device_id_type=pl.DeviceIdType.MESH)
    for d in range(1, m):
        pl.semaphore_signal(barrier, inc=1, device_id=to_lon(d), device_id_type=pl.DeviceIdType.MESH)
    pl.semaphore_wait(barrier, n - 1 + m - 1)
    pending = []

    def halo(field, cols, up, down, side, ss, rs):
        copies = [
            send(field.at[LAT_DEV - 1], up, ss.at[0], rs.at[0], to_lat(1)),
            send(field.at[0], down, ss.at[1], rs.at[1], to_lat(n - 1)),
            send(cols.at[1], side.at[0], ss.at[2], rs.at[2], to_lon(1)),
            send(cols.at[0], side.at[1], ss.at[3], rs.at[3], to_lon(m - 1)),
        ]
        pending.extend(copies)
        return copies

    def landed(copies):
        for copy in copies:
            copy.wait_recv()

    halos = halo(g_ref, gc_ref, hu, hd, hc, h_s, h_r)
    if mode == "first":
        own = own_ref.shape[1] // LANES
        for j in range(own):
            own_all[z, j] = own_ref[:, j * LANES : (j + 1) * LANES]
        owners = [send(own_all.at[z], own_all.at[z], o_s.at[d], o_r.at[d], to_lon(d)) for d in range(1, m)]
        pending.extend(owners)
    parts = [
        send(table_ref.at[lax.rem(me + d, n)], ta.at[d], ta_s.at[d], ta_r.at[d], to_lat(d))
        for d in range(1, n)
    ]
    pending.extend(parts)
    smooth = smooth_ref[0:1, :]
    top_keep = (me > 0).astype(F32)
    bottom_keep = (me < n - 1).astype(F32)
    column = lax.broadcasted_iota(jnp.int32, (LON_DEV, LEV), 0)

    def stencil(field, i, above, below, side):
        mid = field[i]
        left = jnp.where(column == 0, side[0, pl.ds(i, 1), :], pltpu.roll(mid, 1, 0))
        right = jnp.where(
            column == LON_DEV - 1, side[1, pl.ds(i, 1), :], pltpu.roll(mid, LON_DEV - 1, 0)
        )
        return mid + smooth * (above + below + left + right - 4.0 * mid)

    def sweep(field, up, down, side, use, acc):
        acc = use(0, stencil(field, 0, up[...] * top_keep, field[1], side), acc)
        inner = LAT_DEV - 2
        group = next(k for k in (5, 4, 3, 2, 1) if inner % k == 0)

        def rows(it, a):
            for k in range(group):
                i = 1 + it * group + k
                a = use(i, stencil(field, i, field[i - 1], field[i + 1], side), a)
            return a

        acc = lax.fori_loop(0, inner // group, rows, acc)
        end = LAT_DEV - 1
        return use(end, stencil(field, end, field[end - 1], down[...] * bottom_keep, side), acc)

    def keep_columns(i, row):
        rc_ref[0, pl.ds(i, 1), :] = row[0:1]
        rc_ref[1, pl.ds(i, 1), :] = row[LON_DEV - 1 : LON_DEV]

    zero = jnp.zeros((LON_DEV, LEV), F32)
    if mode == "first":

        def use(i, row, acc):
            r_out[i] = row
            keep_columns(i, row)
            return acc + row * row

    else:

        def use(i, row, acc):
            p = p_ref[i]
            q = p + row
            q_ref[i] = q
            return acc + p * q

    def scatter_sum():
        landed(parts)
        total = table_ref[me]
        for d in range(1, n):
            total = total + ta[d]
        bb[z] = total
        across = [send(bb.at[z], bb.at[z], b_s.at[d], b_r.at[d], to_lon(d)) for d in range(1, m)]
        pending.extend(across)
        return across

    def everywhere(buf, tile, ss, rs):
        buf[me] = tile
        copies = [send(buf.at[me], buf.at[me], ss.at[d], rs.at[d], to_lat(d)) for d in range(1, n)]
        pending.extend(copies)
        return copies

    def summed(buf, count):
        total = buf[0]
        for j in range(1, count):
            total = total + buf[j]
        return total

    def along_lon(buf, tile, ss, rs):
        buf[z] = tile
        copies = [send(buf.at[z], buf.at[z], ss.at[d], rs.at[d], to_lon(d)) for d in range(1, m)]
        pending.extend(copies)
        return copies

    if mode != "first":
        across = scatter_sum()
    landed(halos)
    ones = everywhere(s1, fold(sweep(g_ref, hu, hd, hc, use, zero)), s1_s, s1_r)
    if mode == "first":
        second = halo(r_out, rc_ref, hu2, hd2, hc2, k_s, k_r)
        across = scatter_sum()
    landed(across)
    gathers = everywhere(tf, summed(bb, m), c_s, c_r)
    landed(ones)
    crossing = along_lon(sc, summed(s1, n), sc_s, sc_r)
    landed(gathers)

    def tab(j):
        return tf[j // chunk, j % chunk]

    def spread(tile):
        return jnp.full((8, LANES), jnp.sum(tile), F32)

    rz_bias = jnp.zeros((8, LANES), F32)
    rr_bias = jnp.zeros((8, LANES), F32)
    if mode == "first":
        landed(owners)
        for j in range(width):
            rb = tab(j)
            bp = own_all[j // own, j % own]
            diag = bp + tab(width + j)
            pb = rb / diag
            rb_out[j], bp_out[j], diag_out[j], pb_out[j] = rb, bp, diag, pb
            rz_bias = rz_bias + rb * pb
            rr_bias = rr_bias + rb * rb
        rz_bias, rr_bias = spread(rz_bias), spread(rr_bias)
        landed(crossing)
        state_sum = spread(summed(sc, m))
        scal_out[...] = jnp.zeros(scal_out.shape, F32)
        scal_out[0] = state_sum + rz_bias
        scal_out[1] = state_sum + rr_bias
        landed(second)

        def use_u(i, row, acc):
            u_out[i] = row
            return acc

        sweep(r_out, hu2, hd2, hc2, use_u, 0)
    else:
        curve = jnp.zeros((8, LANES), F32)
        for j in range(width):
            pb = pb_ref[j]
            curve = curve + pb * (bp_ref[j] * pb + tab(j))
        curve = spread(curve)
        landed(crossing)
        alpha = scal_ref[0] / (spread(summed(sc, m)) + curve)
        line = alpha[0:1, :]

        def update(it, acc):
            for k in range(4):
                i = it * 4 + k
                row = r_ref[i] - line * q_ref[i]
                if mode == "middle":
                    r_out[i] = row
                    keep_columns(i, row)
                acc = acc + row * row
            return acc

        twos = everywhere(s2, fold(lax.fori_loop(0, LAT_DEV // 4, update, zero)), s2_s, s2_r)
        if mode == "middle":
            second = halo(r_out, rc_ref, hu2, hd2, hc2, k_s, k_r)
        for j in range(width):
            pb = pb_ref[j]
            rb = rb_ref[j] - alpha * (bp_ref[j] * pb + tab(j))
            zb = rb / diag_ref[j]
            if mode == "middle":
                rb_out[j] = rb
                x_out[j] = alpha * pb
            rz_bias = rz_bias + rb * zb
            rr_bias = rr_bias + rb * rb
        rz_bias, rr_bias = spread(rz_bias), spread(rr_bias)
        landed(twos)
        threes = along_lon(s3, summed(s2, n), s3_s, s3_r)
        if mode == "last":
            own = bias_out.shape[1] // LANES
            for j in range(own):
                bias_out[:, j * LANES : (j + 1) * LANES] = (
                    xb_ref[z * own + j] + alpha * pb_ref[z * own + j]
                )
        landed(threes)
        state_sum = spread(summed(s3, m))
        rz_new = state_sum + rz_bias
        scal_out[...] = scal_ref[...]
        scal_out[0] = rz_new
        scal_out[1 + turn] = state_sum + rr_bias
        scal_out[1 + ITERS + turn] = alpha
        if mode == "last":
            lane = lax.broadcasted_iota(jnp.int32, (8, LANES), 1)
            norms = jnp.zeros((8, LANES), F32)
            for j in range(ITERS + 1):
                norms = jnp.where(lane == j, scal_out[1 + j], norms)
            norms_out[...] = jnp.sqrt(norms)
        if mode == "middle":
            beta = rz_new / scal_ref[0]
            slope = beta[0:1, :]
            for j in range(width):
                pb_out[j] = rb_out[j] / diag_ref[j] + beta * pb_ref[j]
            landed(second)

            def use_u(i, row, acc):
                u_out[i] = row + slope * u_ref[i]
                p_out[i] = r_out[i] + slope * p_ref[i]
                return acc

            sweep(r_out, hu2, hd2, hc2, use_u, 0)
    for copy in pending:
        copy.wait_send()


VM = pl.BlockSpec(memory_space=pltpu.VMEM)
SM = pl.BlockSpec(memory_space=pltpu.SMEM)


def shaped(*shape):
    return jax.ShapeDtypeStruct(shape, F32)


def body(
    innovations,
    obs_precision,
    jacobian,
    predictors,
    obs_column,
    obs_channel,
    obs_count,
    smoothing,
    bias_precision,
):
    n = lax.axis_size("swath")
    m = lax.axis_size("chan")
    owned_width = bias_precision.shape[1]
    own = owned_width // LANES
    width = own * m
    blocks = owned_width * m // CH_BLOCK
    slots = obs_precision.shape[0]
    lines = slots // OBS_BLOCK
    grid_lines = lambda a: a.reshape(lines, OBS_BLOCK)
    cells = grid_lines(obs_column)
    line_rows = cells[:, 0] // LON_DEV
    common = (
        line_rows, obs_count, cells, grid_lines(obs_channel), grid_lines(obs_precision),
        predictors, jacobian,
    )
    field = shaped(LAT_DEV, LON_DEV, LEV)
    cols = shaped(2, LAT_DEV, LEV)
    tab = shaped(width, NPRED, LANES)
    scal = shaped(2 + 2 * ITERS, 8, LANES)
    smooth = smoothing.reshape(1, LEV)

    def local(init, *extra):
        used = (2 if init else 1) * width
        padded = -(-used // n) * n
        acc_rows = (2 if init else 1) * NPRED * blocks
        scratch = [pltpu.VMEM((acc_rows, CH_BLOCK), F32)]
        if not init:
            scratch += [
                pltpu.VMEM((LAT_DEV, LON_DEV, 2 * LEV), BF16),
                pltpu.VMEM((NPRED * blocks, CH_BLOCK), F32),
            ]
        out = pl.pallas_call(
            functools.partial(local_kernel, init, blocks),
            out_shape=(field, cols, shaped(padded, NPRED, LANES)),
            in_specs=[SM, SM] + [VM] * (len(common) - 2 + len(extra)),
            out_specs=(VM, VM, VM),
            scratch_shapes=scratch,
            compiler_params=pltpu.CompilerParams(vmem_limit_bytes=VMEM_LIMIT),
            name="local_first" if init else "local_next",
        )(*common, *extra)
        return out[0], out[1], out[2].reshape(n, padded // n, NPRED, LANES)

    def comm(mode, ident, outs, table, *args):
        chunk = table.shape[1]
        sem = lambda k: [pltpu.SemaphoreType.DMA((k,)), pltpu.SemaphoreType.DMA((k,))]
        vm = lambda *s: pltpu.VMEM(s, F32)
        scratch = [
            vm(n, chunk, NPRED, LANES), vm(n, chunk, NPRED, LANES), vm(m, chunk, NPRED, LANES),
            vm(n, 8, LANES), vm(m, 8, LANES), vm(LON_DEV, LEV), vm(LON_DEV, LEV), vm(2, LAT_DEV, LEV),
        ] + sem(n) + sem(4) + sem(n) + sem(m) + sem(n) + sem(m)
        if mode == "first":
            scratch += [vm(m, own, NPRED, LANES)] + sem(m)
        if mode != "first":
            scratch += [vm(LAT_DEV, LON_DEV, LEV), vm(n, 8, LANES), vm(m, 8, LANES)] + sem(n) + sem(m)
        if mode != "last":
            scratch += [vm(LON_DEV, LEV), vm(LON_DEV, LEV), vm(2, LAT_DEV, LEV)] + sem(4)
        return pl.pallas_call(
            functools.partial(comm_kernel, n, m, width, mode, ident),
            out_shape=outs,
            in_specs=[VM] * (4 + len(args)),
            out_specs=jax.tree.map(lambda _: VM, outs),
            scratch_shapes=scratch,
            compiler_params=pltpu.CompilerParams(
                collective_id=ident, has_side_effects=True, vmem_limit_bytes=VMEM_LIMIT
            ),
            name="comm_" + mode,
        )(smooth, *grads, table, *args)

    g, gc, table = local(True, grid_lines(innovations))
    grads = (g, gc)
    r, _, u, rb, diag, bp, pb, sc = comm(
        "first", 0, (field, cols, field, tab, tab, tab, tab, scal), table, bias_precision
    )
    p = r
    state = None
    total = None
    for turn in range(1, ITERS + 1):
        g, gc, table = local(False, u, pb)
        grads = (g, gc)
        args = (p, r, pb, rb, diag, bp, sc)
        old_p = p
        if turn < ITERS:
            outs = (field, cols, field, field, tab, tab, scal, tab)
            r, _, p, u, rb, pb, sc, total = comm("middle", turn, outs, table, *args, u)
        else:
            outs = (scal, shaped(8, LANES), shaped(NPRED, owned_width))
            sc, norms, bias = comm("last", turn, outs, table, *args, total)
        length = sc[1 + ITERS + turn, 0]
        state = length * old_p if state is None else state + length * old_p
    return (state, bias, norms[0, : ITERS + 1])


def solution(mesh):
    placed = (
        P(("swath", "chan")),
        P(("swath", "chan")),
        P(("swath", "chan"), None),
        P(None, ("swath", "chan")),
        P(("swath", "chan")),
        P(("swath", "chan")),
        P("swath", "chan"),
        P(),
        P(None, "chan"),
    )
    return jax.shard_map(
        body,
        mesh=mesh,
        in_specs=placed,
        out_specs=(P("swath", "chan", None), P(None, "chan"), P()),
        check_vma=False,
    )
```

profile of v0, /device:TPU:0, one launch (start us, length us, event | category | flops | bytes accessed | tf_op | source)
XLA Modules:
  0.0 130.1 jit_solution(2013120723297214589)
XLA Ops:
  0.6 0.0 copy-start.10
  0.6 0.0 copy-start.5
  1.3 0.9 slice_reduce_fusion
  2.3 0.0 copy-start
  2.3 2.2 %copy-done = bf16[16384,128]{1,0:T(8,128)(2,1)S(1)} copy-done((bf16[16384,128]{1,0:T(8,128)(2,1)S(1)}, bf16[16384,128]{1,0:T(8,128)(2,1)}, u32[]{:S(2)}) %copy-start) | copy-done | bytes 4194328
  4.5 0.0 copy-start.2
  4.5 1.0 copy-done.2
  5.5 0.0 copy-start.4
  5.5 0.8 copy-done.4
  6.4 0.0 copy-start.6
  6.4 0.8 copy-done.6
  7.2 0.0 copy-start.7
  7.2 0.8 copy-done.7
  8.1 0.0 copy-start.8
  8.1 0.8 copy-done.8
  8.9 0.0 copy-start.9
  8.9 0.0 copy-start.1
  8.9 0.0 copy-start.3
  8.9 11.3 %local_first.1 = (f32[32,64,128]{2,1,0:T(8,128)S(1)}, f32[2,32,128]{2,1,0:T(8,128)S(1)}, f32[80,8,128]{2,1,0:T(8,128)S(1)}) custom-call(s32[128]{0:T(128)S(1)} %and_select_fusion.rows_ref, s32[1,1]{1,0:T(1,128)S(6)} %copy.13.count_ref, s32[128,128]{1,0:T(8,128)S(1)} %bitcast.15, s32[128,128]{1,0:T(8,128)S(1)} %bitcast.18, f32[128,128]{1,0:T(8,128)S(1)} %bitcast.21, ...), custom_call_target="tpu_custom_call" | custom-call | tf_op jit(solution)/shard_map/local_first/pallas_call | solution.py:473
  20.2 0.0 copy-done.10
  20.2 0.0 copy-done.9
  20.2 23.5 %comm_first.1 = (f32[32,64,128]{2,1,0:T(8,128)S(1)}, f32[2,32,128]{2,1,0:T(8,128)}, f32[32,64,128]{2,1,0:T(8,128)S(1)}, f32[40,8,128]{2,1,0:T(8,128)S(1)}, f32[4...) custom-call(f32[1,128]{1,0:T(1,128)S(1)} %bitcast.28, ...), custom_call_target="tpu_custom_call" | custom-call | tf_op jit(solution)/shard_map/comm_first/pallas_call | solution.py:498
  43.8 0.0 copy-done.5
  43.8 0.0 copy-done.1
  43.8 0.0 copy-done.3
  43.8 18.5 %local_next.2 = (f32[32,64,128]{2,1,0:T(8,128)S(1)}, f32[2,32,128]{2,1,0:T(8,128)S(1)}, f32[40,8,128]{2,1,0:T(8,128)S(1)}) custom-call(s32[128]{0:T(128)S(1)} %and_select_fusion.rows_ref, s32[1,1]{1,0:T(1,128)S(6)} %copy.13.count_ref, s32[128,128]{1,0:T(8,128)S(1)} %bitcast.16, s32[128,128]{1,0:T(8,128)S(1)} %bitcast.19, f32[128,128]{1,0:T(8,128)S(1)} %bitcast.22, ...), custom_call_target="tpu_custom_call" | custom-call | tf_op jit(solution)/shard_map/local_next/pallas_call | solution.py:473
  62.3 25.2 %comm_middle.1 = (f32[32,64,128]{2,1,0:T(8,128)S(1)}, f32[2,32,128]{2,1,0:T(8,128)}, f32[32,64,128]{2,1,0:T(8,128)S(1)}, f32[32,64,128]{2,1,0:T(8,128)S(1)}, f32...) custom-call(f32[1,128]{1,0:T(1,128)S(1)} %bitcast.29, ...), custom_call_target="tpu_custom_call" | custom-call | tf_op jit(solution)/shard_map/comm_middle/pallas_call | solution.py:498
  87.5 18.5 %local_next.3 = (f32[32,64,128]{2,1,0:T(8,128)S(1)}, f32[2,32,128]{2,1,0:T(8,128)S(1)}, f32[40,8,128]{2,1,0:T(8,128)S(1)}) custom-call(s32[128]{0:T(128)S(1)} %and_select_fusion.rows_ref, s32[1,1]{1,0:T(1,128)S(6)} %copy.13.count_ref, s32[128,128]{1,0:T(8,128)S(1)} %bitcast.17, s32[128,128]{1,0:T(8,128)S(1)} %bitcast.20, f32[128,128]{1,0:T(8,128)S(1)} %bitcast.23, ...), custom_call_target="tpu_custom_call" | custom-call | tf_op jit(solution)/shard_map/local_next/pallas_call | solution.py:473
  106.0 21.8 %comm_last.1 = (f32[6,8,128]{2,1,0:T(8,128)S(1)}, f32[8,128]{1,0:T(8,128)S(1)}, f32[8,1280]{1,0:T(8,128)S(1)}) custom-call(f32[1,128]{1,0:T(1,128)S(1)} %bitcast.30, f32[32,64,128]{2,1,0:T(8,128)S(1)} %get-tuple-element.45.refs_1_, f32[2,32,128]{2,1,0:T(8,128)S(1)} %get-tuple-element.46.refs_2_, f32[8,5,8,128]{3,2,1,0:T(8,128)S(1)} %bitcast.25, ...), custom_call_target="tpu_custom_call" | custom-call | tf_op jit(solution)/shard_map/comm_last/pallas_call | solution.py:498
  127.8 1.2 multiply_add_fusion
  129.0 0.5 slice_bitcast_fusion
  129.5 0.6 copy.14
  (2 shorter events, 0.0 us)
Async XLA Ops:
  0.6 19.6 %copy-start.10 = (f32[128]{0:T(128)S(1)}, f32[128]{0:T(128)}, u32[]{:S(2)}) copy-start(f32[128]{0:T(128)} %param.16) | copy-start | bytes 1540
  0.6 43.1 %copy-start.5 = (s32[16384]{0:T(1024)S(1)}, s32[16384]{0:T(1024)}, u32[]{:S(2)}) copy-start(s32[16384]{0:T(1024)} %param.13) | copy-start | bytes 196612
  2.3 2.2 %copy-start = (bf16[16384,128]{1,0:T(8,128)(2,1)S(1)}, bf16[16384,128]{1,0:T(8,128)(2,1)}, u32[]{:S(2)}) copy-start(bf16[16384,128]{1,0:T(8,128)(2,1)} %jac_ref.5) | copy-start | bytes 12582916
  4.5 1.0 copy-start.2
  5.5 0.8 copy-start.4
  6.4 0.8 copy-start.6
  7.2 0.8 copy-start.7
  8.1 0.8 copy-start.8
  8.9 11.3 %copy-start.9 = (f32[8,1280]{1,0:T(8,128)S(1)}, f32[8,1280]{1,0:T(8,128)}, u32[]{:S(2)}) copy-start(f32[8,1280]{1,0:T(8,128)} %refs_4_.1) | copy-start | bytes 122884
  8.9 34.9 %copy-start.1 = (bf16[16384,128]{1,0:T(8,128)(2,1)S(1)}, bf16[16384,128]{1,0:T(8,128)(2,1)}, u32[]{:S(2)}) copy-start(bf16[16384,128]{1,0:T(8,128)(2,1)} %jac_ref.5) | copy-start | bytes 12582916
  8.9 34.9 %copy-start.3 = (f32[8,16384]{1,0:T(8,128)S(1)}, f32[8,16384]{1,0:T(8,128)}, u32[]{:S(2)}) copy-start(f32[8,16384]{1,0:T(8,128)} %pred_ref.5) | copy-start | bytes 1572868
where the time goes:
time: 131 us; the launch traced here: 130 us
  Pallas kernels  119 us (91%)
  local copies, waits for them, and re-layouts  8.68 us (7%)
  between operations  1.45 us (1%)
    pallas_call x3, Pallas kernels, comm(): pl.pallas_call(functools.partial(comm_kernel, n, m, width, mode, ident),...  70.5 us
    pallas_call x3, Pallas kernels, local(): pl.pallas_call(functools.partial(local_kernel, init, blocks), out_shape=(...  48.3 us
    unnamed x23, local copies, waits for them, and re-layouts  7.22 us

commit v1 on v0

v1 whole, which is shorter than its diff:
```python
import functools

import jax
import jax.numpy as jnp
from jax import lax
from jax.experimental import pallas as pl
from jax.experimental.pallas import tpu as pltpu
from jax.sharding import PartitionSpec as P

LEV = 128
NPRED = 8
CH_BLOCK = 256
OBS_BLOCK = 128
LAT_DEV = 32
LON_DEV = 64
ITERS = 2
LINES = 8
PAIRS = LINES // 2
PAIR = 2 * OBS_BLOCK
LANES = 128
TILE = (8, LANES)
F32 = jnp.float32
BF16 = jnp.bfloat16
NT = (((1,), (1,)), ((), ()))
VMEM_LIMIT = 60 * 1024 * 1024


def halves(value):
    high = value.astype(BF16)
    return high, (value - high.astype(F32)).astype(BF16)


def fold(value):
    total = value[0:8]
    for i in range(1, value.shape[0] // 8):
        total = total + value[8 * i : 8 * i + 8]
    return total


def total_of(parts):
    total = parts[0]
    for part in parts[1:]:
        total = total + part
    return total


def kernel(n, m, own, blocks, lines, chunk, *refs):
    refs = list(refs)
    take = lambda k: [refs.pop(0) for _ in range(k)]
    count_ref, smooth_ref, bprec_ref = take(3)
    cell_h, chan_h, prec_h, innov_h, pred_h, jac_h = take(6)
    x_out, bias_out, norms_out = take(3)
    cell_ref, chan_ref, prec_ref, innov_ref, pred_ref, jac_ref = take(6)
    hot_ref, msk_ref, w_ref, y_ref, f_ref, part_ref = take(6)
    index_v, index_s = take(2)
    g_ref, gc_ref, r0_ref, r1_ref, p1_ref, rc_ref, split_ref = take(7)
    acc_ref, table_ref, coef_ref = take(3)
    bp_c, diag_c, r_c, p_c, own_all = take(5)
    hu, hd, hc, ta, bb, tf, sz, sw = take(8)
    in_s, ix_s, o_s, o_r, h_s, h_r, ta_s, ta_r, b_s, b_r, c_s, c_r, z_s, z_r, w_s, w_r = take(16)
    width = own * m
    groups = lines // LINES
    me = lax.axis_index("swath")
    z = lax.axis_index("chan")
    per = CH_BLOCK // LANES

    def to_lat(d):
        return {"swath": lax.rem(me + d, n)}

    def to_lon(d):
        return {"chan": lax.rem(z + d, m)}

    pending = []

    def send(src, dst, ss, rs, dev):
        copy = pltpu.make_async_remote_copy(
            src_ref=src, dst_ref=dst, send_sem=ss, recv_sem=rs,
            device_id=dev, device_id_type=pl.DeviceIdType.MESH,
        )
        copy.start()
        pending.append(copy)
        return copy

    def landed(copies):
        for copy in copies:
            copy.wait_recv()

    barrier = pltpu.get_barrier_semaphore()
    for d in range(1, n):
        pl.semaphore_signal(barrier, inc=1, device_id=to_lat(d), device_id_type=pl.DeviceIdType.MESH)
    for d in range(1, m):
        pl.semaphore_signal(barrier, inc=1, device_id=to_lon(d), device_id_type=pl.DeviceIdType.MESH)

    loads = []
    for k, (src, dst) in enumerate((
        (chan_h, chan_ref), (prec_h, prec_ref), (pred_h, pred_ref),
        (innov_h, innov_ref), (cell_h, cell_ref), (jac_h, jac_ref),
    )):
        copy = pltpu.make_async_copy(src, dst, in_s.at[k])
        copy.start()
        loads.append(copy)
    load_chan, load_prec, load_pred, load_innov, load_cell, load_jac = loads

    count = count_ref[0, 0]
    sub = lax.broadcasted_iota(jnp.int32, TILE, 0)
    slot8 = sub * OBS_BLOCK + lax.broadcasted_iota(jnp.int32, TILE, 1)

    def pairs_of(tile):
        return [
            jnp.concatenate([tile[2 * p : 2 * p + 1], tile[2 * p + 1 : 2 * p + 2]], axis=1)
            for p in range(PAIRS)
        ]

    def stack_left(term, mask):
        high = term.astype(BF16).astype(F32)
        low = term - high
        sides = []
        for side in (high, low):
            twice = jnp.concatenate([side, side], axis=0).astype(BF16)
            sides.append(jnp.concatenate([twice] * (blocks // 2), axis=0) * mask)
        return jnp.concatenate(sides, axis=0)

    def add_table(lefts, hots):
        acc_ref[...] += lax.dot_general(
            jnp.concatenate(lefts, axis=1), jnp.concatenate(hots, axis=1), NT,
            preferred_element_type=F32,
        )

    def preds_of(it, p):
        start = pl.multiple_of((it * PAIRS + p) * PAIR, PAIR)
        return pred_ref[:, pl.ds(start, PAIR)]

    def write_table(s):
        half = NPRED * blocks
        for j in range(n * chunk):
            if j < width:
                top = (j // per) * NPRED
                lanes = slice((j % per) * LANES, (j % per + 1) * LANES)
                tile = acc_ref[top : top + NPRED, lanes] + acc_ref[half + top : half + top + NPRED, lanes]
            else:
                tile = jnp.zeros((NPRED, LANES), F32)
            table_ref[s, j // chunk, j % chunk] = tile

    def scatter(s):
        return [
            send(table_ref.at[s, lax.rem(me + d, n)], ta.at[s, d], ta_s.at[s, d], ta_r.at[s, d], to_lat(d))
            for d in range(1, n)
        ]

    def across(s, copies):
        landed(copies)
        bb[s, z] = total_of([table_ref[s, me]] + [ta[s, d] for d in range(1, n)])
        return [
            send(bb.at[s, z], bb.at[s, z], b_s.at[s, d], b_r.at[s, d], to_lon(d)) for d in range(1, m)
        ]

    def chunk_sum(s, copies):
        landed(copies)
        return total_of([bb[s, j] for j in range(m)])

    def gather(i, value):
        tf[i, me] = value
        return [
            send(tf.at[i, me], tf.at[i, me], c_s.at[i, d], c_r.at[i, d], to_lat(d)) for d in range(1, n)
        ]

    def lon_tile(e, tile):
        sz[e, z] = tile
        return [send(sz.at[e, z], sz.at[e, z], z_s.at[e, d], z_r.at[e, d], to_lon(d)) for d in range(1, m)]

    def lon_total(e, copies):
        landed(copies)
        return total_of([sz[e, j] for j in range(m)])

    def lat_tile(e, tile):
        sw[e, me] = tile
        return [send(sw.at[e, me], sw.at[e, me], w_s.at[e, d], w_r.at[e, d], to_lat(d)) for d in range(1, n)]

    def lat_total(e, copies):
        landed(copies)
        return jnp.sum(total_of([sw[e, j] for j in range(n)]), axis=1, keepdims=True)

    def rows_tile(*tiles):
        out = jnp.zeros(TILE, F32)
        for k, tile in enumerate(tiles):
            out = jnp.where(sub == k, jnp.sum(tile, axis=0, keepdims=True), out)
        return out

    def halo(k, field, cols):
        return [
            send(field.at[LAT_DEV - 1], hu.at[k], h_s.at[k, 0], h_r.at[k, 0], to_lat(1)),
            send(field.at[0], hd.at[k], h_s.at[k, 1], h_r.at[k, 1], to_lat(n - 1)),
            send(cols.at[1], hc.at[k, 0], h_s.at[k, 2], h_r.at[k, 2], to_lon(1)),
            send(cols.at[0], hc.at[k, 1], h_s.at[k, 3], h_r.at[k, 3], to_lon(m - 1)),
        ]

    load_chan.wait()
    load_prec.wait()
    load_pred.wait()
    load_innov.wait()
    acc_ref[...] = jnp.zeros_like(acc_ref)
    iota_ch = lax.broadcasted_iota(jnp.int32, (CH_BLOCK, PAIR), 0)
    iota_b = lax.broadcasted_iota(jnp.int32, (NPRED * blocks, PAIR), 0) // NPRED

    def square_step(it, carry):
        base = pl.multiple_of(it * LINES, LINES)
        w8 = jnp.where(base * OBS_BLOCK + slot8 < count, prec_ref[pl.ds(base, LINES), :], 0.0)
        w_ref[pl.ds(base, LINES), :] = w8
        y_ref[pl.ds(base, LINES), :] = w8 * innov_ref[pl.ds(base, LINES), :]
        weights = pairs_of(w8)
        chans = pairs_of(chan_ref[pl.ds(base, LINES), :])
        lefts, hots = [], []
        for p in range(PAIRS):
            hot = jnp.where(iota_ch == chans[p] % CH_BLOCK, 1.0, 0.0).astype(BF16)
            mask = jnp.where(iota_b == chans[p] // CH_BLOCK, 1.0, 0.0).astype(BF16)
            hot_ref[it * PAIRS + p] = hot
            msk_ref[it * PAIRS + p] = mask
            preds = preds_of(it, p)
            lefts.append(stack_left(preds * preds * weights[p], mask))
            hots.append(hot)
        add_table(lefts, hots)
        return carry

    lax.fori_loop(0, groups, square_step, 0)
    write_table(0)

    load_cell.wait()
    first = jnp.broadcast_to(cell_ref[:, 0:1], (lines, LANES)) // LON_DEV
    iota_l = lax.broadcasted_iota(jnp.int32, (lines, LANES), 0)
    iota_r = lax.broadcasted_iota(jnp.int32, (lines, LANES), 1)
    turned = jnp.transpose(first)
    before = jnp.where((first == turned) & (iota_l < iota_r), iota_l, -1)
    before = jnp.max(before, axis=0, keepdims=True)
    last = jnp.max(jnp.where(first == iota_r, iota_l, -1), axis=0, keepdims=True)
    index_v[0:1, :] = turned[0:1, :]
    index_v[1:2, :] = jnp.where(before < 0, lines, before)
    index_v[2:3, :] = jnp.where(last < 0, lines, last)
    load_index = pltpu.make_async_copy(index_v, index_s, ix_s.at[0])
    load_index.start()

    pl.semaphore_wait(barrier, n - 1 + m - 1)
    for j in range(own):
        own_all[z, j] = bprec_ref[:, j * LANES : (j + 1) * LANES]
    squares = scatter(0)
    owners = [send(own_all.at[z], own_all.at[z], o_s.at[d], o_r.at[d], to_lon(d)) for d in range(1, m)]

    def adjoint_bias(s):
        acc_ref[...] = jnp.zeros_like(acc_ref)

        def table_step(it, carry):
            base = pl.multiple_of(it * LINES, LINES)
            values = pairs_of(y_ref[pl.ds(base, LINES), :])
            lefts, hots = [], []
            for p in range(PAIRS):
                lefts.append(stack_left(preds_of(it, p) * values[p], msk_ref[it * PAIRS + p]))
                hots.append(hot_ref[it * PAIRS + p])
            add_table(lefts, hots)
            return carry

        lax.fori_loop(0, groups, table_step, 0)
        write_table(s)
        return scatter(s)

    iota_col = lax.broadcasted_iota(jnp.int32, (LON_DEV, OBS_BLOCK), 0)

    def jac_of(line):
        return jac_ref[pl.ds(pl.multiple_of(line * OBS_BLOCK, OBS_BLOCK), OBS_BLOCK), :]

    def adjoint_state(k):
        def line_step(it, carry):
            base = pl.multiple_of(it * LINES, LINES)
            cols = cell_ref[pl.ds(base, LINES), :] % LON_DEV
            values = y_ref[pl.ds(base, LINES), :]
            outs = []
            for l in range(LINES):
                high, low = halves(jnp.where(iota_col == cols[l : l + 1, :], values[l : l + 1, :], 0.0))
                jac = jac_of(base + l)
                outs.append(jnp.dot(
                    jnp.concatenate([high, low], axis=1), jnp.concatenate([jac, jac], axis=0),
                    preferred_element_type=F32,
                ))
            for l in range(LINES):
                part_ref[base + l] = outs[l] + part_ref[index_s[1, base + l]]
            return carry

        lax.fori_loop(0, groups, line_step, 0)

        def row_step(i, carry):
            row = part_ref[index_s[2, i]]
            g_ref[k, i] = row
            gc_ref[k, 0, pl.ds(i, 1), :] = row[0:1, :]
            gc_ref[k, 1, pl.ds(i, 1), :] = row[LON_DEV - 1 : LON_DEV, :]
            return carry

        lax.fori_loop(0, LAT_DEV, row_step, 0)
        return halo(2 * k, g_ref.at[k], gc_ref.at[k])

    smooth = smooth_ref[0:1, :]
    top_keep = (me > 0).astype(F32)
    bottom_keep = (me < n - 1).astype(F32)
    column = lax.broadcasted_iota(jnp.int32, (LON_DEV, LEV), 0)
    zero = jnp.zeros((LON_DEV, LEV), F32)

    def sweep(field, k, use, acc):
        up, down, side = hu.at[k], hd.at[k], hc.at[k]

        def stencil(i, above, below):
            mid = field[i]
            left = jnp.where(column == 0, side[0, pl.ds(i, 1), :], pltpu.roll(mid, 1, 0))
            right = jnp.where(
                column == LON_DEV - 1, side[1, pl.ds(i, 1), :], pltpu.roll(mid, LON_DEV - 1, 0)
            )
            return mid + smooth * (above + below + left + right - 4.0 * mid)

        acc = use(0, stencil(0, up[...] * top_keep, field[1]), acc)
        inner = LAT_DEV - 2
        group = next(k for k in (5, 4, 3, 2, 1) if inner % k == 0)

        def rows(it, a):
            for k in range(group):
                i = 1 + it * group + k
                a = use(i, stencil(i, field[i - 1], field[i + 1]), a)
            return a

        acc = lax.fori_loop(0, inner // group, rows, acc)
        end = LAT_DEV - 1
        return use(end, stencil(end, field[end - 1], down[...] * bottom_keep), acc)

    def keep_columns(k, i, row):
        rc_ref[k, 0, pl.ds(i, 1), :] = row[0:1]
        rc_ref[k, 1, pl.ds(i, 1), :] = row[LON_DEV - 1 : LON_DEV]

    def forward_state(field, k, old):
        def use(i, row, acc):
            high, low = halves(row)
            split_ref[i] = jnp.concatenate([high, low], axis=1)
            return acc

        sweep(field, k, use, 0)

        def line_step(it, carry):
            base = pl.multiple_of(it * LINES, LINES)
            cols = cell_ref[pl.ds(base, LINES), :] % LON_DEV
            seen = []
            for l in range(LINES):
                jac = jac_of(base + l)
                both = lax.dot_general(
                    split_ref[index_s[0, base + l]], jnp.concatenate([jac, jac], axis=1), NT,
                    preferred_element_type=F32,
                )
                seen.append(jnp.sum(jnp.where(iota_col == cols[l : l + 1, :], both, 0.0), axis=0, keepdims=True))
            y_ref[pl.ds(base, LINES), :] = jnp.concatenate(seen, axis=0)
            return carry

        lax.fori_loop(0, groups, line_step, 0)

    def forward_bias(i, beta):
        for b in range(blocks):
            for h in range(per):
                j = b * per + h
                high, low = halves(tf[i, j // chunk, j % chunk])
                coef_ref[b * NPRED : (b + 1) * NPRED, h * LANES : (h + 1) * LANES] = high
                coef_ref[b * NPRED : (b + 1) * NPRED, CH_BLOCK + h * LANES : CH_BLOCK + (h + 1) * LANES] = low
        coef2 = coef_ref[...]

        def look_step(it, acc):
            base = pl.multiple_of(it * LINES, LINES)
            chans = pairs_of(chan_ref[pl.ds(base, LINES), :])
            looked = []
            for p in range(PAIRS):
                hot = hot_ref[it * PAIRS + p]
                mid = jnp.dot(coef2, jnp.concatenate([hot, hot], axis=0), preferred_element_type=F32)
                which = jnp.broadcast_to(chans[p] // CH_BLOCK, (NPRED, PAIR))
                total = jnp.zeros((NPRED, PAIR), F32)
                for b in range(blocks):
                    total = total + jnp.where(which == b, mid[b * NPRED : (b + 1) * NPRED], 0.0)
                total = jnp.sum(total * preds_of(it, p), axis=0, keepdims=True)
                looked += [total[:, :OBS_BLOCK], total[:, OBS_BLOCK:]]
            f8 = y_ref[pl.ds(base, LINES), :] + jnp.concatenate(looked, axis=0)
            if beta is not None:
                f8 = f8 + beta * f_ref[pl.ds(base, LINES), :]
            y8 = w_ref[pl.ds(base, LINES), :] * f8
            f_ref[pl.ds(base, LINES), :] = f8
            y_ref[pl.ds(base, LINES), :] = y8
            return acc + y8 * f8

        return lax.fori_loop(0, groups, look_step, jnp.zeros(TILE, F32))

    def spread(column):
        return jnp.broadcast_to(column, TILE)

    def dots(*pairs):
        return [total_of([a[j] * b[j] for j in range(chunk)]) for a, b in pairs]

    part_ref[lines] = zero
    sums = adjoint_bias(1)
    squares = across(0, squares)
    load_index.wait()
    load_jac.wait()
    halos = adjoint_state(0)
    sums = across(1, sums)
    landed(halos)

    def use_first(i, row, acc):
        r0_ref[i] = row
        keep_columns(0, i, row)
        return acc + row * row

    pp_state = fold(sweep(g_ref.at[0], 0, use_first, zero))
    halos = halo(1, r0_ref, rc_ref.at[0])
    crossing = lon_tile(0, pp_state)
    landed(owners)
    for j in range(chunk):
        spot = jnp.minimum(me * chunk + j, width - 1)
        bp_c[j] = own_all[spot // own, lax.rem(spot, own)]
    diag_c[...] = bp_c[...] + chunk_sum(0, squares)
    r_c[...] = chunk_sum(1, sums)
    p_c[...] = r_c[...] / diag_c[...]
    gathers = gather(0, p_c[...])
    around = lat_tile(0, rows_tile(lon_total(0, crossing), *dots((r_c, p_c), (r_c, r_c))))
    landed(halos)
    forward_state(r0_ref, 1, None)
    landed(gathers)
    totals = lat_total(0, around)
    rz = spread(totals[0:1] + totals[1:2])
    norms = [spread(totals[0:1] + totals[2:3])]
    beta = None
    alphas = []
    for turn in range(ITERS):
        final = turn == ITERS - 1
        observed = forward_bias(turn, None if beta is None else beta[0:1])
        sums = adjoint_bias(2 + turn)
        if turn > 0:
            slope = beta[0:1]

            def p_step(it, acc):
                for k in range(4):
                    i = it * 4 + k
                    row = r1_ref[i] + slope * r0_ref[i]
                    p1_ref[i] = row
                    acc = acc + row * row
                return acc

            pp_state = fold(lax.fori_loop(0, LAT_DEV // 4, p_step, zero))
            p_c[...] = tf[turn, me] + beta * p_c[...]
        crossing = lon_tile(1 + 2 * turn, pp_state + observed)
        halos = adjoint_state(1 + turn)
        pp_bias = total_of([bp_c[j] * p_c[j] * p_c[j] for j in range(chunk)])
        around = lat_tile(1 + 2 * turn, rows_tile(lon_total(1 + 2 * turn, crossing), pp_bias))
        sums = across(2 + turn, sums)
        totals = lat_total(1 + 2 * turn, around)
        alpha = rz / spread(totals[0:1] + totals[1:2])
        alphas.append(alpha)
        line = alpha[0:1]
        landed(halos)
        p_ref, old_ref = (p1_ref, r1_ref) if turn > 0 else (r0_ref, r0_ref)

        def use_next(i, row, acc):
            new = old_ref[i] - line * (p_ref[i] + row)
            if not final:
                r1_ref[i] = new
                keep_columns(1, i, new)
            return acc + new * new

        rr_state = fold(sweep(g_ref.at[1 + turn], 2 + 2 * turn, use_next, zero))
        crossing = lon_tile(2 + 2 * turn, rr_state)
        if not final:
            halos = halo(3 + 2 * turn, r1_ref, rc_ref.at[1])
        image = bp_c[...] * p_c[...] + chunk_sum(2 + turn, sums)
        r_c[...] = r_c[...] - alpha * image
        z_c = r_c[...] / diag_c[...]
        if not final:
            gathers = gather(turn + 1, z_c)
        around = lat_tile(
            2 + 2 * turn, rows_tile(lon_total(2 + 2 * turn, crossing), *dots((r_c, z_c), (r_c, r_c)))
        )
        if not final:
            landed(halos)
            forward_state(r1_ref, 3 + 2 * turn, None)
            landed(gathers)
        else:
            first_line, last_line = alphas[0][0:1], alphas[1][0:1]

            def x_step(it, carry):
                for k in range(4):
                    i = it * 4 + k
                    x_out[i] = first_line * r0_ref[i] + last_line * p1_ref[i]
                return carry

            lax.fori_loop(0, LAT_DEV // 4, x_step, 0)
            for j in range(own):
                spot = z * own + j
                row, col = spot // chunk, lax.rem(spot, chunk)
                start = tf[0, row, col]
                bias_out[:, j * LANES : (j + 1) * LANES] = alphas[0] * start + alphas[1] * (
                    tf[1, row, col] + beta * start
                )
        totals = lat_total(2 + 2 * turn, around)
        new = spread(totals[0:1] + totals[1:2])
        norms.append(spread(totals[0:1] + totals[2:3]))
        beta = new / rz
        rz = new
    lane = lax.broadcasted_iota(jnp.int32, TILE, 1)
    squares = jnp.zeros(TILE, F32)
    for j in range(ITERS + 1):
        squares = jnp.where(lane == j, norms[j], squares)
    norms_out[...] = jnp.sqrt(squares)
    for copy in pending:
        copy.wait_send()


def shaped(*shape):
    return jax.ShapeDtypeStruct(shape, F32)


def body(
    innovations,
    obs_precision,
    jacobian,
    predictors,
    obs_column,
    obs_channel,
    obs_count,
    smoothing,
    bias_precision,
):
    n = lax.axis_size("swath")
    m = lax.axis_size("chan")
    owned_width = bias_precision.shape[1]
    own = owned_width // LANES
    width = own * m
    blocks = owned_width * m // CH_BLOCK
    slots = obs_precision.shape[0]
    lines = slots // OBS_BLOCK
    chunk = -(-width // n)
    half = NPRED * blocks
    grid_lines = lambda a: a.reshape(lines, OBS_BLOCK)
    vm = lambda *s: pltpu.VMEM(s, F32)
    vb = lambda *s: pltpu.VMEM(s, BF16)
    vi = lambda *s: pltpu.VMEM(s, jnp.int32)
    sem = lambda *s: pltpu.SemaphoreType.DMA(s)
    halos = 1 + 2 * ITERS
    tables = 2 + ITERS
    events = 1 + 2 * ITERS
    scratch = [
        vi(lines, OBS_BLOCK), vi(lines, OBS_BLOCK), vm(lines, OBS_BLOCK), vm(lines, OBS_BLOCK),
        vm(NPRED, slots), vb(slots, LEV),
        vb(lines // 2, CH_BLOCK, PAIR), vb(lines // 2, half, PAIR),
        vm(lines, OBS_BLOCK), vm(lines, OBS_BLOCK), vm(lines, OBS_BLOCK), vm(lines + 1, LON_DEV, LEV),
        vi(8, LANES), pltpu.SMEM((8, LANES), jnp.int32),
        vm(1 + ITERS, LAT_DEV, LON_DEV, LEV), vm(1 + ITERS, 2, LAT_DEV, LEV),
        vm(LAT_DEV, LON_DEV, LEV), vm(LAT_DEV, LON_DEV, LEV), vm(LAT_DEV, LON_DEV, LEV),
        vm(2, 2, LAT_DEV, LEV), vb(LAT_DEV, LON_DEV, 2 * LEV),
        vm(2 * half, CH_BLOCK), vm(tables, n, chunk, NPRED, LANES), vb(half, 2 * CH_BLOCK),
        vm(chunk, NPRED, LANES), vm(chunk, NPRED, LANES), vm(chunk, NPRED, LANES),
        vm(chunk, NPRED, LANES), vm(m, own, NPRED, LANES),
        vm(halos, LON_DEV, LEV), vm(halos, LON_DEV, LEV), vm(halos, 2, LAT_DEV, LEV),
        vm(tables, n, chunk, NPRED, LANES), vm(tables, m, chunk, NPRED, LANES),
        vm(ITERS, n, chunk, NPRED, LANES), vm(events, m, 8, LANES), vm(events, n, 8, LANES),
        sem(6), sem(1), sem(m), sem(m), sem(halos, 4), sem(halos, 4), sem(tables, n), sem(tables, n),
        sem(tables, m), sem(tables, m), sem(ITERS, n), sem(ITERS, n), sem(events, m), sem(events, m),
        sem(events, n), sem(events, n),
    ]
    VM = pl.BlockSpec(memory_space=pltpu.VMEM)
    HB = pl.BlockSpec(memory_space=pltpu.HBM)
    x, bias, norms = pl.pallas_call(
        functools.partial(kernel, n, m, own, blocks, lines, chunk),
        out_shape=(shaped(LAT_DEV, LON_DEV, LEV), shaped(NPRED, owned_width), shaped(8, LANES)),
        in_specs=[pl.BlockSpec(memory_space=pltpu.SMEM), VM, VM] + [HB] * 6,
        out_specs=(VM, VM, VM),
        scratch_shapes=scratch,
        compiler_params=pltpu.CompilerParams(
            collective_id=0, has_side_effects=True, vmem_limit_bytes=VMEM_LIMIT
        ),
        name="cg",
    )(
        obs_count, smoothing.reshape(1, LEV), bias_precision,
        grid_lines(obs_column), grid_lines(obs_channel), grid_lines(obs_precision),
        grid_lines(innovations), predictors, jacobian,
    )
    return (x, bias, norms[0, : ITERS + 1])


def solution(mesh):
    placed = (
        P(("swath", "chan")),
        P(("swath", "chan")),
        P(("swath", "chan"), None),
        P(None, ("swath", "chan")),
        P(("swath", "chan")),
        P(("swath", "chan")),
        P("swath", "chan"),
        P(),
        P(None, "chan"),
    )
    return jax.shard_map(
        body,
        mesh=mesh,
        in_specs=placed,
        out_specs=(P("swath", "chan", None), P(None, "chan"), P()),
        check_vma=False,
    )
```

time: 131 us -> 104 us (0.79)
  Pallas kernels: 119 us -> 97.7 us
  local copies, waits for them, and re-layouts: 8.68 us -> 4.89 us
    pallas_call x6 -> x1, Pallas kernels: 119 us -> 97.7 us  [body(): pl.pallas_call(functools.partial(kernel, n, m, own, blocks, lines, chunk)...]
    unnamed x23 -> x2, local copies, waits for them, and re-layouts: 7.22 us -> 3.7 us
where the time goes in v1:
time: 104 us
  Pallas kernels  97.7 us (94%)
  local copies, waits for them, and re-layouts  4.89 us (5%)
  between operations  1.29 us (1%)
    pallas_call x1, Pallas kernels, body(): pl.pallas_call(functools.partial(kernel, n, m, own, blocks, lines, chunk)...  97.7 us
    unnamed x2, local copies, waits for them, and re-layouts  3.7 us

profile of v1, /device:TPU:0, one launch (start us, length us, event | category | flops | bytes accessed | tf_op | source)
XLA Modules:
  0.0 103.9 jit_solution(5304408261705422093)
XLA Ops:
  1.3 97.7 %cg.1 = (f32[32,64,128]{2,1,0:T(8,128)}, f32[8,1280]{1,0:T(8,128)}, f32[8,128]{1,0:T(8,128)}) custom-call(s32[1,1]{1,0:T(1,128)S(6)} %copy.14.refs_0_, f32[1,128]{1,0:T(1,128)} %bitcast.11, f32[8,1280]{1,0:T(8,128)} %refs_2_.1, s32[128,128]{1,0:T(8,128)} %bitcast.7, s32[128,128]{1,0:T(8,128)} %bitcast.8, f32[128,128]{1,0:T(8,128)} %bitcast.9, ...), custom_call_target="tpu_custom_call" | custom-call | tf_op jit(solution)/shard_map/cg/pallas_call | solution.py:566
  99.0 1.2 %slice_bitcast_fusion = f32[3]{0:T(128)} fusion(f32[8,128]{1,0:T(8,128)} %get-tuple-element.8), kind=kLoop, calls=%fused_computation | loop fusion | bytes 24 | tf_op jit(solution)/shard_map/squeeze | solution.py:581
  100.2 2.3 %copy.15 = f32[32,64,128]{2,1,0:T(8,128)} copy(f32[32,64,128]{2,1,0:T(8,128)} %get-tuple-element.12) | data formatting | bytes 2097152
  102.5 1.4 %copy.16 = f32[8,1280]{1,0:T(8,128)} copy(f32[8,1280]{1,0:T(8,128)} %get-tuple-element.13) | data formatting | bytes 81920

commit v2 on v1

--- a/solution.py
+++ b/solution.py
@@ -16,13 +16,14 @@
 ITERS = 2
 LINES = 8
 PAIRS = LINES // 2
+SQUARE_STEP, TABLE_STEP, LOOK_STEP, ADJOINT_STEP, FORWARD_STEP = 2, 4, 4, 4, 4
 PAIR = 2 * OBS_BLOCK
 LANES = 128
 TILE = (8, LANES)
 F32 = jnp.float32
 BF16 = jnp.bfloat16
 NT = (((1,), (1,)), ((), ()))
-VMEM_LIMIT = 60 * 1024 * 1024
+VMEM_LIMIT = 44 * 1024 * 1024
 
 
 def halves(value):
@@ -42,6 +43,10 @@
     for part in parts[1:]:
         total = total + part
     return total
+
+
+def stage(name, run, *args):
+    return run(*args)
 
 
 def kernel(n, m, own, blocks, lines, chunk, *refs):
@@ -51,7 +56,7 @@
     cell_h, chan_h, prec_h, innov_h, pred_h, jac_h = take(6)
     x_out, bias_out, norms_out = take(3)
     cell_ref, chan_ref, prec_ref, innov_ref, pred_ref, jac_ref = take(6)
-    hot_ref, msk_ref, w_ref, y_ref, f_ref, part_ref = take(6)
+    turned_ref, hot_ref, msk_ref, w_ref, y_ref, f_ref, part_ref = take(7)
     index_v, index_s = take(2)
     g_ref, gc_ref, r0_ref, r1_ref, p1_ref, rc_ref, split_ref = take(7)
     acc_ref, table_ref, coef_ref = take(3)
@@ -81,9 +86,12 @@
         pending.append(copy)
         return copy
 
-    def landed(copies):
+    def await_all(copies):
         for copy in copies:
             copy.wait_recv()
+
+    def landed(copies):
+        stage("wait", await_all, copies)
 
     barrier = pltpu.get_barrier_semaphore()
     for d in range(1, n):
@@ -110,6 +118,10 @@
             jnp.concatenate([tile[2 * p : 2 * p + 1], tile[2 * p + 1 : 2 * p + 2]], axis=1)
             for p in range(PAIRS)
         ]
+
+    def rows_of(row, count):
+        packed = jnp.broadcast_to(row, (16, row.shape[1])).astype(BF16)
+        return jnp.concatenate([packed] * (count // 16), axis=0)
 
     def stack_left(term, mask):
         high = term.astype(BF16).astype(F32)
@@ -197,32 +209,37 @@
     load_chan.wait()
     load_prec.wait()
     load_pred.wait()
-    load_innov.wait()
+    stage("load", load_innov.wait)
     acc_ref[...] = jnp.zeros_like(acc_ref)
-    iota_ch = lax.broadcasted_iota(jnp.int32, (CH_BLOCK, PAIR), 0)
-    iota_b = lax.broadcasted_iota(jnp.int32, (NPRED * blocks, PAIR), 0) // NPRED
-
-    def square_step(it, carry):
-        base = pl.multiple_of(it * LINES, LINES)
-        w8 = jnp.where(base * OBS_BLOCK + slot8 < count, prec_ref[pl.ds(base, LINES), :], 0.0)
-        w_ref[pl.ds(base, LINES), :] = w8
-        y_ref[pl.ds(base, LINES), :] = w8 * innov_ref[pl.ds(base, LINES), :]
-        weights = pairs_of(w8)
-        chans = pairs_of(chan_ref[pl.ds(base, LINES), :])
+    iota_ch = lax.broadcasted_iota(jnp.int32, (CH_BLOCK, PAIR), 0).astype(F32).astype(BF16)
+    iota_b = (lax.broadcasted_iota(jnp.int32, (NPRED * blocks, PAIR), 0) // NPRED).astype(F32).astype(BF16)
+    one, none = jnp.ones((), BF16), jnp.zeros((), BF16)
+
+    def square_step(step, carry):
         lefts, hots = [], []
-        for p in range(PAIRS):
-            hot = jnp.where(iota_ch == chans[p] % CH_BLOCK, 1.0, 0.0).astype(BF16)
-            mask = jnp.where(iota_b == chans[p] // CH_BLOCK, 1.0, 0.0).astype(BF16)
-            hot_ref[it * PAIRS + p] = hot
-            msk_ref[it * PAIRS + p] = mask
-            preds = preds_of(it, p)
-            lefts.append(stack_left(preds * preds * weights[p], mask))
-            hots.append(hot)
+        for g in range(SQUARE_STEP):
+            it = step * SQUARE_STEP + g
+            base = pl.multiple_of(it * LINES, LINES)
+            w8 = jnp.where(base * OBS_BLOCK + slot8 < count, prec_ref[pl.ds(base, LINES), :], 0.0)
+            w_ref[pl.ds(base, LINES), :] = w8
+            y_ref[pl.ds(base, LINES), :] = w8 * innov_ref[pl.ds(base, LINES), :]
+            weights = pairs_of(w8)
+            chan8 = chan_ref[pl.ds(base, LINES), :]
+            lows = pairs_of((chan8 % CH_BLOCK).astype(F32))
+            tops = pairs_of((chan8 // CH_BLOCK).astype(F32))
+            for p in range(PAIRS):
+                hot = jnp.where(iota_ch == rows_of(lows[p], CH_BLOCK), one, none)
+                mask = jnp.where(iota_b == rows_of(tops[p], NPRED * blocks), one, none)
+                hot_ref[it * PAIRS + p] = hot
+                msk_ref[it * PAIRS + p] = mask
+                preds = preds_of(it, p)
+                lefts.append(stack_left(preds * preds * weights[p], mask))
+                hots.append(hot)
         add_table(lefts, hots)
         return carry
 
-    lax.fori_loop(0, groups, square_step, 0)
-    write_table(0)
+    stage("squares", lax.fori_loop, 0, groups // SQUARE_STEP, square_step, 0)
+    stage("write", write_table, 0)
 
     load_cell.wait()
     first = jnp.broadcast_to(cell_ref[:, 0:1], (lines, LANES)) // LON_DEV
@@ -238,7 +255,7 @@
     load_index = pltpu.make_async_copy(index_v, index_s, ix_s.at[0])
     load_index.start()
 
-    pl.semaphore_wait(barrier, n - 1 + m - 1)
+    stage("barrier", pl.semaphore_wait, barrier, n - 1 + m - 1)
     for j in range(own):
         own_all[z, j] = bprec_ref[:, j * LANES : (j + 1) * LANES]
     squares = scatter(0)
@@ -247,18 +264,19 @@
     def adjoint_bias(s):
         acc_ref[...] = jnp.zeros_like(acc_ref)
 
-        def table_step(it, carry):
-            base = pl.multiple_of(it * LINES, LINES)
-            values = pairs_of(y_ref[pl.ds(base, LINES), :])
+        def table_step(step, carry):
             lefts, hots = [], []
-            for p in range(PAIRS):
-                lefts.append(stack_left(preds_of(it, p) * values[p], msk_ref[it * PAIRS + p]))
-                hots.append(hot_ref[it * PAIRS + p])
+            for g in range(TABLE_STEP):
+                it = step * TABLE_STEP + g
+                values = pairs_of(y_ref[pl.ds(pl.multiple_of(it * LINES, LINES), LINES), :])
+                for p in range(PAIRS):
+                    lefts.append(stack_left(preds_of(it, p) * values[p], msk_ref[it * PAIRS + p]))
+                    hots.append(hot_ref[it * PAIRS + p])
             add_table(lefts, hots)
             return carry
 
-        lax.fori_loop(0, groups, table_step, 0)
-        write_table(s)
+        stage("table", lax.fori_loop, 0, groups // TABLE_STEP, table_step, 0)
+        stage("write", write_table, s)
         return scatter(s)
 
     iota_col = lax.broadcasted_iota(jnp.int32, (LON_DEV, OBS_BLOCK), 0)
@@ -267,23 +285,29 @@
         return jac_ref[pl.ds(pl.multiple_of(line * OBS_BLOCK, OBS_BLOCK), OBS_BLOCK), :]
 
     def adjoint_state(k):
-        def line_step(it, carry):
-            base = pl.multiple_of(it * LINES, LINES)
-            cols = cell_ref[pl.ds(base, LINES), :] % LON_DEV
-            values = y_ref[pl.ds(base, LINES), :]
+        def line_step(step, carry):
             outs = []
-            for l in range(LINES):
-                high, low = halves(jnp.where(iota_col == cols[l : l + 1, :], values[l : l + 1, :], 0.0))
-                jac = jac_of(base + l)
-                outs.append(jnp.dot(
-                    jnp.concatenate([high, low], axis=1), jnp.concatenate([jac, jac], axis=0),
-                    preferred_element_type=F32,
-                ))
-            for l in range(LINES):
-                part_ref[base + l] = outs[l] + part_ref[index_s[1, base + l]]
+            for g in range(ADJOINT_STEP):
+                base = pl.multiple_of((step * ADJOINT_STEP + g) * LINES, LINES)
+                cols = cell_ref[pl.ds(base, LINES), :] % LON_DEV
+                values = y_ref[pl.ds(base, LINES), :]
+                for l in range(0, LINES, 2):
+                    rows = []
+                    for j in (l, l + 1):
+                        high, low = halves(jnp.where(iota_col == cols[j : j + 1, :], values[j : j + 1, :], 0.0))
+                        rows.append(jnp.concatenate([high, low], axis=1))
+                    jacs = jnp.concatenate([jac_of(base + l), jac_of(base + l + 1)], axis=1)
+                    both = jnp.dot(
+                        jnp.concatenate(rows, axis=0), jnp.concatenate([jacs, jacs], axis=0),
+                        preferred_element_type=F32,
+                    )
+                    outs += [both[:LON_DEV, :LEV], both[LON_DEV:, LEV:]]
+            first_line = step * ADJOINT_STEP * LINES
+            for l in range(ADJOINT_STEP * LINES):
+                part_ref[first_line + l] = outs[l] + part_ref[index_s[1, first_line + l]]
             return carry
 
-        lax.fori_loop(0, groups, line_step, 0)
+        stage("adjoint", lax.fori_loop, 0, groups // ADJOINT_STEP, line_step, 0)
 
         def row_step(i, carry):
             row = part_ref[index_s[2, i]]
@@ -292,7 +316,7 @@
             gc_ref[k, 1, pl.ds(i, 1), :] = row[LON_DEV - 1 : LON_DEV, :]
             return carry
 
-        lax.fori_loop(0, LAT_DEV, row_step, 0)
+        stage("rows", lax.fori_loop, 0, LAT_DEV, row_step, 0)
         return halo(2 * k, g_ref.at[k], gc_ref.at[k])
 
     smooth = smooth_ref[0:1, :]
@@ -336,23 +360,27 @@
             split_ref[i] = jnp.concatenate([high, low], axis=1)
             return acc
 
-        sweep(field, k, use, 0)
-
-        def line_step(it, carry):
-            base = pl.multiple_of(it * LINES, LINES)
-            cols = cell_ref[pl.ds(base, LINES), :] % LON_DEV
-            seen = []
-            for l in range(LINES):
-                jac = jac_of(base + l)
-                both = lax.dot_general(
-                    split_ref[index_s[0, base + l]], jnp.concatenate([jac, jac], axis=1), NT,
-                    preferred_element_type=F32,
-                )
-                seen.append(jnp.sum(jnp.where(iota_col == cols[l : l + 1, :], both, 0.0), axis=0, keepdims=True))
-            y_ref[pl.ds(base, LINES), :] = jnp.concatenate(seen, axis=0)
+        stage("sweep_u", sweep, field, k, use, 0)
+
+        def line_step(step, carry):
+            for g in range(FORWARD_STEP):
+                base = pl.multiple_of((step * FORWARD_STEP + g) * LINES, LINES)
+                cols = cell_ref[pl.ds(base, LINES), :] % LON_DEV
+                seen = []
+                for l in range(0, LINES, 2):
+                    fields = [split_ref[index_s[0, base + j]] for j in (l, l + 1)]
+                    jacs = jnp.concatenate([turned_ref[base + l], turned_ref[base + l + 1]], axis=1)
+                    both = jnp.dot(
+                        jnp.concatenate(fields, axis=0), jnp.concatenate([jacs, jacs], axis=0),
+                        preferred_element_type=F32,
+                    )
+                    for j, part in ((l, both[:LON_DEV, :OBS_BLOCK]), (l + 1, both[LON_DEV:, OBS_BLOCK:])):
+                        picked = jnp.where(iota_col == cols[j : j + 1, :], part, 0.0)
+                        seen.append(jnp.sum(picked, axis=0, keepdims=True))
+                y_ref[pl.ds(base, LINES), :] = jnp.concatenate(seen, axis=0)
             return carry
 
-        lax.fori_loop(0, groups, line_step, 0)
+        stage("forward", lax.fori_loop, 0, groups // FORWARD_STEP, line_step, 0)
 
     def forward_bias(i, beta):
         for b in range(blocks):
@@ -363,28 +391,31 @@
                 coef_ref[b * NPRED : (b + 1) * NPRED, CH_BLOCK + h * LANES : CH_BLOCK + (h + 1) * LANES] = low
         coef2 = coef_ref[...]
 
-        def look_step(it, acc):
-            base = pl.multiple_of(it * LINES, LINES)
-            chans = pairs_of(chan_ref[pl.ds(base, LINES), :])
-            looked = []
-            for p in range(PAIRS):
-                hot = hot_ref[it * PAIRS + p]
-                mid = jnp.dot(coef2, jnp.concatenate([hot, hot], axis=0), preferred_element_type=F32)
-                which = jnp.broadcast_to(chans[p] // CH_BLOCK, (NPRED, PAIR))
-                total = jnp.zeros((NPRED, PAIR), F32)
-                for b in range(blocks):
-                    total = total + jnp.where(which == b, mid[b * NPRED : (b + 1) * NPRED], 0.0)
-                total = jnp.sum(total * preds_of(it, p), axis=0, keepdims=True)
-                looked += [total[:, :OBS_BLOCK], total[:, OBS_BLOCK:]]
-            f8 = y_ref[pl.ds(base, LINES), :] + jnp.concatenate(looked, axis=0)
-            if beta is not None:
-                f8 = f8 + beta * f_ref[pl.ds(base, LINES), :]
-            y8 = w_ref[pl.ds(base, LINES), :] * f8
-            f_ref[pl.ds(base, LINES), :] = f8
-            y_ref[pl.ds(base, LINES), :] = y8
-            return acc + y8 * f8
-
-        return lax.fori_loop(0, groups, look_step, jnp.zeros(TILE, F32))
+        def look_step(step, acc):
+            for g in range(LOOK_STEP):
+                it = step * LOOK_STEP + g
+                base = pl.multiple_of(it * LINES, LINES)
+                tops = pairs_of(chan_ref[pl.ds(base, LINES), :] // CH_BLOCK)
+                looked = []
+                for p in range(PAIRS):
+                    hot = hot_ref[it * PAIRS + p]
+                    mid = jnp.dot(coef2, jnp.concatenate([hot, hot], axis=0), preferred_element_type=F32)
+                    which = jnp.broadcast_to(tops[p], (NPRED, PAIR))
+                    total = jnp.zeros((NPRED, PAIR), F32)
+                    for b in range(blocks):
+                        total = jnp.where(which == b, mid[b * NPRED : (b + 1) * NPRED], total)
+                    total = jnp.sum(total * preds_of(it, p), axis=0, keepdims=True)
+                    looked += [total[:, :OBS_BLOCK], total[:, OBS_BLOCK:]]
+                f8 = y_ref[pl.ds(base, LINES), :] + jnp.concatenate(looked, axis=0)
+                if beta is not None:
+                    f8 = f8 + beta * f_ref[pl.ds(base, LINES), :]
+                y8 = w_ref[pl.ds(base, LINES), :] * f8
+                f_ref[pl.ds(base, LINES), :] = f8
+                y_ref[pl.ds(base, LINES), :] = y8
+                acc = acc + y8 * f8
+            return acc
+
+        return stage("look", lax.fori_loop, 0, groups // LOOK_STEP, look_step, jnp.zeros(TILE, F32))
 
     def spread(column):
         return jnp.broadcast_to(column, TILE)
@@ -395,10 +426,17 @@
     part_ref[lines] = zero
     sums = adjoint_bias(1)
     squares = across(0, squares)
-    load_index.wait()
-    load_jac.wait()
+    stage("load_index", load_index.wait)
+    stage("load_jac", load_jac.wait)
     halos = adjoint_state(0)
     sums = across(1, sums)
+
+    def turn_step(it, carry):
+        for l in range(LINES):
+            turned_ref[it * LINES + l] = jnp.transpose(jac_of(it * LINES + l))
+        return carry
+
+    stage("turn", lax.fori_loop, 0, groups, turn_step, 0)
     landed(halos)
 
     def use_first(i, row, acc):
@@ -406,7 +444,7 @@
         keep_columns(0, i, row)
         return acc + row * row
 
-    pp_state = fold(sweep(g_ref.at[0], 0, use_first, zero))
+    pp_state = fold(stage("sweep", sweep, g_ref.at[0], 0, use_first, zero))
     halos = halo(1, r0_ref, rc_ref.at[0])
     crossing = lon_tile(0, pp_state)
     landed(owners)
@@ -441,7 +479,7 @@
                     acc = acc + row * row
                 return acc
 
-            pp_state = fold(lax.fori_loop(0, LAT_DEV // 4, p_step, zero))
+            pp_state = fold(stage("p_step", lax.fori_loop, 0, LAT_DEV // 4, p_step, zero))
             p_c[...] = tf[turn, me] + beta * p_c[...]
         crossing = lon_tile(1 + 2 * turn, pp_state + observed)
         halos = adjoint_state(1 + turn)
@@ -462,7 +500,7 @@
                 keep_columns(1, i, new)
             return acc + new * new
 
-        rr_state = fold(sweep(g_ref.at[1 + turn], 2 + 2 * turn, use_next, zero))
+        rr_state = fold(stage("sweep", sweep, g_ref.at[1 + turn], 2 + 2 * turn, use_next, zero))
         crossing = lon_tile(2 + 2 * turn, rr_state)
         if not final:
             halos = halo(3 + 2 * turn, r1_ref, rc_ref.at[1])
@@ -487,7 +525,7 @@
                     x_out[i] = first_line * r0_ref[i] + last_line * p1_ref[i]
                 return carry
 
-            lax.fori_loop(0, LAT_DEV // 4, x_step, 0)
+            stage("x_step", lax.fori_loop, 0, LAT_DEV // 4, x_step, 0)
             for j in range(own):
                 spot = z * own + j
                 row, col = spot // chunk, lax.rem(spot, chunk)
@@ -507,6 +545,18 @@
     norms_out[...] = jnp.sqrt(squares)
     for copy in pending:
         copy.wait_send()
+
+
+def publish(x_ref, bias_ref, norms_ref, x_out, bias_out, norms_out, row_ref, sems):
+    row_ref[...] = norms_ref[0, : row_ref.shape[0]]
+    copies = [
+        pltpu.make_async_copy(src, dst, sems.at[k])
+        for k, (src, dst) in enumerate(((x_ref, x_out), (bias_ref, bias_out), (row_ref, norms_out)))
+    ]
+    for copy in copies:
+        copy.start()
+    for copy in copies:
+        copy.wait()
 
 
 def shaped(*shape):
@@ -535,6 +585,7 @@
     chunk = -(-width // n)
     half = NPRED * blocks
     grid_lines = lambda a: a.reshape(lines, OBS_BLOCK)
+    held = lambda a: pltpu.with_memory_space_constraint(a, pltpu.HBM)
     vm = lambda *s: pltpu.VMEM(s, F32)
     vb = lambda *s: pltpu.VMEM(s, BF16)
     vi = lambda *s: pltpu.VMEM(s, jnp.int32)
@@ -545,7 +596,7 @@
     scratch = [
         vi(lines, OBS_BLOCK), vi(lines, OBS_BLOCK), vm(lines, OBS_BLOCK), vm(lines, OBS_BLOCK),
         vm(NPRED, slots), vb(slots, LEV),
-        vb(lines // 2, CH_BLOCK, PAIR), vb(lines // 2, half, PAIR),
+        vb(lines, LEV, OBS_BLOCK), vb(lines // 2, CH_BLOCK, PAIR), vb(lines // 2, half, PAIR),
         vm(lines, OBS_BLOCK), vm(lines, OBS_BLOCK), vm(lines, OBS_BLOCK), vm(lines + 1, LON_DEV, LEV),
         vi(8, LANES), pltpu.SMEM((8, LANES), jnp.int32),
         vm(1 + ITERS, LAT_DEV, LON_DEV, LEV), vm(1 + ITERS, 2, LAT_DEV, LEV),
@@ -574,11 +625,20 @@
         ),
         name="cg",
     )(
-        obs_count, smoothing.reshape(1, LEV), bias_precision,
-        grid_lines(obs_column), grid_lines(obs_channel), grid_lines(obs_precision),
-        grid_lines(innovations), predictors, jacobian,
+        obs_count, held(smoothing.reshape(1, LEV)), held(bias_precision),
+        held(grid_lines(obs_column)), held(grid_lines(obs_channel)), held(grid_lines(obs_precision)),
+        held(grid_lines(innovations)), held(predictors), held(jacobian),
     )
-    return (x, bias, norms[0, : ITERS + 1])
+    kept = (x.shape, bias.shape, (ITERS + 1,))
+    return pl.pallas_call(
+        publish,
+        out_shape=tuple(shaped(*shape) for shape in kept),
+        in_specs=[VM, VM, VM],
+        out_specs=(HB, HB, HB),
+        scratch_shapes=[vm(ITERS + 1), sem(3)],
+        compiler_params=pltpu.CompilerParams(vmem_limit_bytes=4 * 1024 * 1024),
+        name="publish",
+    )(x, bias, norms)
 
 
 def solution(mesh):

time: 104 us -> 75.3 us (0.72)
  Pallas kernels: 97.7 us -> 73.9 us
  local copies, waits for them, and re-layouts: 4.89 us -> 0 us
    pallas_call x1, Pallas kernels: 97.7 us -> 72.9 us  [body(): pl.pallas_call(functools.partial(kernel, n, m, own, blocks, lines, chunk)...]
    unnamed x2 -> x0, local copies, waits for them, and re-layouts: 3.7 us -> none
    squeeze x1 -> x0, local copies, waits for them, and re-layouts: 1.19 us -> none  [body(): return (x, bias, norms[0, :ITERS + 1])]
where the time goes in v2:
time: 75.3 us; the launch traced here: 75.1 us
  Pallas kernels  73.9 us (98%)
  between operations  1.29 us (2%)
    pallas_call x1, Pallas kernels, body(): pl.pallas_call(functools.partial(kernel, n, m, own, blocks, lines, chunk)...  72.9 us

profile of v2, /device:TPU:0, one launch (start us, length us, event | category | flops | bytes accessed | tf_op | source)
XLA Modules:
  0.0 75.1 jit_solution(7975000989678227524)
XLA Ops:
  1.3 72.9 %cg.1 = (f32[32,64,128]{2,1,0:T(8,128)S(1)}, f32[8,1280]{1,0:T(8,128)S(1)}, f32[8,128]{1,0:T(8,128)S(1)}) custom-call(s32[1,1]{1,0:T(1,128)S(6)} %copy.12.refs_0_, f32[1,128]{1,0:T(1,128)} %bitcast.9, f32[8,1280]{1,0:T(8,128)} %refs_2_.1, s32[128,128]{1,0:T(8,128)} %bitcast.5, s32[128,128]{1,0:T(8,128)} %bitcast.6, f32[128,128]{1,0:T(8,128)} %bitcast.7, ...), custom_call_target="tpu_custom_call" | custom-call | tf_op jit(solution)/shard_map/cg/pallas_call | solution.py:617
  74.1 1.0 %publish.1 = (f32[32,64,128]{2,1,0:T(8,128)}, f32[8,1280]{1,0:T(8,128)}, f32[3]{0:T(128)}) custom-call(f32[32,64,128]{2,1,0:T(8,128)S(1)} %get-tuple-element.6.x_ref, f32[8,1280]{1,0:T(8,128)S(1)} %get-tuple-element.7.bias_ref, f32[8,128]{1,0:T(8,128)S(1)} %get-tuple-element.8.norms_ref), custom_call_target="tpu_custom_call" | custom-call | tf_op jit(solution)/shard_map/publish/pallas_call | solution.py:633

commit v3 on v2

--- a/solution.py
+++ b/solution.py
@@ -16,9 +16,10 @@
 ITERS = 2
 LINES = 8
 PAIRS = LINES // 2
-SQUARE_STEP, TABLE_STEP, LOOK_STEP, ADJOINT_STEP, FORWARD_STEP = 2, 4, 4, 4, 4
+SQUARE_STEP, TABLE_STEP, LOOK_STEP, ADJOINT_STEP, FORWARD_STEP = 4, 8, 8, 4, 4
 PAIR = 2 * OBS_BLOCK
 LANES = 128
+PIECES = 2
 TILE = (8, LANES)
 F32 = jnp.float32
 BF16 = jnp.bfloat16
@@ -58,16 +59,19 @@
     cell_ref, chan_ref, prec_ref, innov_ref, pred_ref, jac_ref = take(6)
     turned_ref, hot_ref, msk_ref, w_ref, y_ref, f_ref, part_ref = take(7)
     index_v, index_s = take(2)
-    g_ref, gc_ref, r0_ref, r1_ref, p1_ref, rc_ref, split_ref = take(7)
+    g_ref, gc_ref, r0_ref, r1_ref, p1_ref, q_ref, s_ref, kept_ref, split_ref = take(9)
     acc_ref, table_ref, coef_ref = take(3)
-    bp_c, diag_c, r_c, p_c, own_all = take(5)
-    hu, hd, hc, ta, bb, tf, sz, sw = take(8)
+    bp_c, diag_c, r_c, p_c, z_c, q_c, own_ref = take(7)
+    hv, hc, hx, rim_rows, rim_cols, ta, bb, tf, sz, sw = take(10)
     in_s, ix_s, o_s, o_r, h_s, h_r, ta_s, ta_r, b_s, b_r, c_s, c_r, z_s, z_r, w_s, w_r = take(16)
     width = own * m
     groups = lines // LINES
     me = lax.axis_index("swath")
     z = lax.axis_index("chan")
     per = CH_BLOCK // LANES
+    count = min(PIECES, chunk)
+    cuts = [chunk * k // count for k in range(count + 1)]
+    pieces = [pl.ds(a, b - a) for a, b in zip(cuts, cuts[1:])]
 
     def to_lat(d):
         return {"swath": lax.rem(me + d, n)}
@@ -83,8 +87,14 @@
             device_id=dev, device_id_type=pl.DeviceIdType.MESH,
         )
         copy.start()
-        pending.append(copy)
-        return copy
+
+    def sent(ref, ss, rs):
+        group = pltpu.make_async_remote_copy(
+            src_ref=ref, dst_ref=ref, send_sem=ss, recv_sem=rs,
+            device_id=to_lon(1), device_id_type=pl.DeviceIdType.MESH,
+        )
+        pending.append(group)
+        return group
 
     def await_all(copies):
         for copy in copies:
@@ -93,11 +103,20 @@
     def landed(copies):
         stage("wait", await_all, copies)
 
+    def diagonal(d, e):
+        return {"swath": lax.rem(me + d, n), "chan": lax.rem(z + e, m)}
+
+    corners = [(1, 1), (1, m - 1), (n - 1, 1), (n - 1, m - 1)]
     barrier = pltpu.get_barrier_semaphore()
     for d in range(1, n):
         pl.semaphore_signal(barrier, inc=1, device_id=to_lat(d), device_id_type=pl.DeviceIdType.MESH)
     for d in range(1, m):
         pl.semaphore_signal(barrier, inc=1, device_id=to_lon(d), device_id_type=pl.DeviceIdType.MESH)
+
+    for d, e in corners:
+        pl.semaphore_signal(
+            barrier, inc=1, device_id=diagonal(d, e), device_id_type=pl.DeviceIdType.MESH
+        )
 
     loads = []
     for k, (src, dst) in enumerate((
@@ -154,31 +173,44 @@
             table_ref[s, j // chunk, j % chunk] = tile
 
     def scatter(s):
-        return [
-            send(table_ref.at[s, lax.rem(me + d, n)], ta.at[s, d], ta_s.at[s, d], ta_r.at[s, d], to_lat(d))
-            for d in range(1, n)
-        ]
-
-    def across(s, copies):
-        landed(copies)
-        bb[s, z] = total_of([table_ref[s, me]] + [ta[s, d] for d in range(1, n)])
-        return [
-            send(bb.at[s, z], bb.at[s, z], b_s.at[s, d], b_r.at[s, d], to_lon(d)) for d in range(1, m)
-        ]
-
-    def chunk_sum(s, copies):
-        landed(copies)
-        return total_of([bb[s, j] for j in range(m)])
-
-    def gather(i, value):
-        tf[i, me] = value
-        return [
-            send(tf.at[i, me], tf.at[i, me], c_s.at[i, d], c_r.at[i, d], to_lat(d)) for d in range(1, n)
-        ]
+        groups = []
+        for k, part in enumerate(pieces):
+            for d in range(1, n):
+                send(
+                    table_ref.at[s, lax.rem(me + d, n), part], ta.at[s, d, part],
+                    ta_s.at[s, k], ta_r.at[s, k], to_lat(d),
+                )
+            groups.append(sent(ta.at[s, pl.ds(1, n - 1), part], ta_s.at[s, k], ta_r.at[s, k]))
+        return groups
+
+    def across(s, arriving, between=None):
+        leaving = []
+        for k, part in enumerate(pieces):
+            if between is not None:
+                between(k)
+            landed([arriving[k]])
+            bb[s, z, part] = total_of([table_ref[s, me, part]] + [ta[s, d, part] for d in range(1, n)])
+            for d in range(1, m):
+                send(bb.at[s, z, part], bb.at[s, z, part], b_s.at[s, k], b_r.at[s, k], to_lon(d))
+            leaving.append(sent(bb.at[s, pl.ds(0, m - 1), part], b_s.at[s, k], b_r.at[s, k]))
+        return leaving
+
+    def chunk_sum(s, k, arriving):
+        landed([arriving[k]])
+        return total_of([bb[s, j, pieces[k]] for j in range(m)])
+
+    def gather(i, k, value):
+        part = pieces[k]
+        tf[i, me, part] = value
+        for d in range(1, n):
+            send(tf.at[i, me, part], tf.at[i, me, part], c_s.at[i, k], c_r.at[i, k], to_lat(d))
+        return [sent(tf.at[i, pl.ds(0, n - 1), part], c_s.at[i, k], c_r.at[i, k])]
 
     def lon_tile(e, tile):
         sz[e, z] = tile
-        return [send(sz.at[e, z], sz.at[e, z], z_s.at[e, d], z_r.at[e, d], to_lon(d)) for d in range(1, m)]
+        for d in range(1, m):
+            send(sz.at[e, z], sz.at[e, z], z_s.at[e], z_r.at[e], to_lon(d))
+        return [sent(sz.at[e, pl.ds(0, m - 1)], z_s.at[e], z_r.at[e])]
 
     def lon_total(e, copies):
         landed(copies)
@@ -186,7 +218,9 @@
 
     def lat_tile(e, tile):
         sw[e, me] = tile
-        return [send(sw.at[e, me], sw.at[e, me], w_s.at[e, d], w_r.at[e, d], to_lat(d)) for d in range(1, n)]
+        for d in range(1, n):
+            send(sw.at[e, me], sw.at[e, me], w_s.at[e], w_r.at[e], to_lat(d))
+        return [sent(sw.at[e, pl.ds(0, n - 1)], w_s.at[e], w_r.at[e])]
 
     def lat_total(e, copies):
         landed(copies)
@@ -198,13 +232,28 @@
             out = jnp.where(sub == k, jnp.sum(tile, axis=0, keepdims=True), out)
         return out
 
-    def halo(k, field, cols):
-        return [
-            send(field.at[LAT_DEV - 1], hu.at[k], h_s.at[k, 0], h_r.at[k, 0], to_lat(1)),
-            send(field.at[0], hd.at[k], h_s.at[k, 1], h_r.at[k, 1], to_lat(n - 1)),
-            send(cols.at[1], hc.at[k, 0], h_s.at[k, 2], h_r.at[k, 2], to_lon(1)),
-            send(cols.at[0], hc.at[k, 1], h_s.at[k, 3], h_r.at[k, 3], to_lon(m - 1)),
+    def halo(k, wide):
+        field, cols = g_ref.at[k], gc_ref.at[k]
+        count = 2 if wide else 1
+        last = pl.ds(LAT_DEV - count, count)
+        near = pl.ds(0, count)
+        far = pl.ds(2 - count, count)
+        moves = [
+            (0, field.at[last], hv.at[k, 0, far], to_lat(1)),
+            (0, field.at[near], hv.at[k, 1, near], to_lat(n - 1)),
+            (1, cols.at[1, far], hc.at[k, 0, far], to_lon(1)),
+            (1, cols.at[0, near], hc.at[k, 1, near], to_lon(m - 1)),
         ]
+        groups = [hv.at[k, pl.ds(0, 2), near], hc.at[k, pl.ds(0, 2), near]]
+        if wide:
+            top, end = pl.ds(0, 1), pl.ds(LAT_DEV - 1, 1)
+            sources = (cols.at[1, 1, end], cols.at[0, 0, end], cols.at[1, 1, top], cols.at[0, 0, top])
+            for q, (src, (d, e)) in enumerate(zip(sources, corners)):
+                moves.append((2, src, hx.at[k, q, top], diagonal(d, e)))
+            groups.append(hx.at[k, pl.ds(0, len(corners)), top])
+        for j, src, dst, dev in moves:
+            send(src, dst, h_s.at[k, j], h_r.at[k, j], dev)
+        return [sent(ref, h_s.at[k, j], h_r.at[k, j]) for j, ref in enumerate(groups)]
 
     load_chan.wait()
     load_prec.wait()
@@ -255,11 +304,24 @@
     load_index = pltpu.make_async_copy(index_v, index_s, ix_s.at[0])
     load_index.start()
 
-    stage("barrier", pl.semaphore_wait, barrier, n - 1 + m - 1)
+    stage("barrier", pl.semaphore_wait, barrier, n - 1 + m - 1 + len(corners))
+    squares = scatter(0)
+    spots = [jnp.minimum(me * chunk + j, width - 1) for j in range(chunk)]
     for j in range(own):
-        own_all[z, j] = bprec_ref[:, j * LANES : (j + 1) * LANES]
-    squares = scatter(0)
-    owners = [send(own_all.at[z], own_all.at[z], o_s.at[d], o_r.at[d], to_lon(d)) for d in range(1, m)]
+        own_ref[j] = bprec_ref[:, j * LANES : (j + 1) * LANES]
+
+    def bias_copy(j, d):
+        return pltpu.make_async_remote_copy(
+            src_ref=own_ref.at[lax.rem(spots[j], own)], dst_ref=bp_c.at[j], send_sem=o_s.at[j],
+            recv_sem=o_r.at[j], device_id=to_lon(d), device_id_type=pl.DeviceIdType.MESH,
+        )
+
+    for j in range(chunk):
+        @pl.when(spots[j] // own == z)
+        def _():
+            for d in range(1, m):
+                bias_copy(j, d).start()
+            bp_c[j] = own_ref[lax.rem(spots[j], own)]
 
     def adjoint_bias(s):
         acc_ref[...] = jnp.zeros_like(acc_ref)
@@ -312,12 +374,13 @@
         def row_step(i, carry):
             row = part_ref[index_s[2, i]]
             g_ref[k, i] = row
-            gc_ref[k, 0, pl.ds(i, 1), :] = row[0:1, :]
-            gc_ref[k, 1, pl.ds(i, 1), :] = row[LON_DEV - 1 : LON_DEV, :]
+            for c in range(2):
+                gc_ref[k, 0, c, pl.ds(i, 1), :] = row[c : c + 1, :]
+                gc_ref[k, 1, c, pl.ds(i, 1), :] = row[LON_DEV - 2 + c : LON_DEV - 1 + c, :]
             return carry
 
         stage("rows", lax.fori_loop, 0, LAT_DEV, row_step, 0)
-        return halo(2 * k, g_ref.at[k], gc_ref.at[k])
+        return halo(k, k < ITERS)
 
     smooth = smooth_ref[0:1, :]
     top_keep = (me > 0).astype(F32)
@@ -325,18 +388,39 @@
     column = lax.broadcasted_iota(jnp.int32, (LON_DEV, LEV), 0)
     zero = jnp.zeros((LON_DEV, LEV), F32)
 
-    def sweep(field, k, use, acc):
-        up, down, side = hu.at[k], hd.at[k], hc.at[k]
-
+    def relaxed(mid, above, below, left, right):
+        return mid + smooth * (above + below + left + right - 4.0 * mid)
+
+    def rim(k):
+        field, cols, side = g_ref.at[k], gc_ref.at[k], hc.at[k]
+        south_west, south_east, north_west, north_east = [hx[k, q, 0:1, :] for q in range(4)]
+        lats = lax.broadcasted_iota(jnp.int32, (LAT_DEV, LEV), 0)
+
+        def row(mid, above, below, west, east, keep):
+            left = jnp.where(column == 0, west, pltpu.roll(mid, 1, 0))
+            right = jnp.where(column == LON_DEV - 1, east, pltpu.roll(mid, LON_DEV - 1, 0))
+            return relaxed(mid, above, below, left, right) * keep
+
+        def col(mid, left, right, north, south):
+            above = jnp.where(lats == 0, north * top_keep, pltpu.roll(mid, 1, 0))
+            below = jnp.where(lats == LAT_DEV - 1, south * bottom_keep, pltpu.roll(mid, LAT_DEV - 1, 0))
+            return relaxed(mid, above, below, left, right)
+
+        rim_rows[0] = row(hv[k, 0, 1], hv[k, 0, 0], field[0], south_west, south_east, top_keep)
+        rim_rows[1] = row(hv[k, 1, 0], field[LAT_DEV - 1], hv[k, 1, 1], north_west, north_east, bottom_keep)
+        rim_cols[0] = col(side[0, 1], side[0, 0], cols[0, 0], south_west, north_west)
+        rim_cols[1] = col(side[1, 0], cols[1, 1], side[1, 1], south_east, north_east)
+
+    def sweep(field, up, down, west, east, use, acc):
         def stencil(i, above, below):
             mid = field[i]
-            left = jnp.where(column == 0, side[0, pl.ds(i, 1), :], pltpu.roll(mid, 1, 0))
+            left = jnp.where(column == 0, west[pl.ds(i, 1), :], pltpu.roll(mid, 1, 0))
             right = jnp.where(
-                column == LON_DEV - 1, side[1, pl.ds(i, 1), :], pltpu.roll(mid, LON_DEV - 1, 0)
+                column == LON_DEV - 1, east[pl.ds(i, 1), :], pltpu.roll(mid, LON_DEV - 1, 0)
             )
-            return mid + smooth * (above + below + left + right - 4.0 * mid)
-
-        acc = use(0, stencil(0, up[...] * top_keep, field[1]), acc)
+            return relaxed(mid, above, below, left, right)
+
+        acc = use(0, stencil(0, up, field[1]), acc)
         inner = LAT_DEV - 2
         group = next(k for k in (5, 4, 3, 2, 1) if inner % k == 0)
 
@@ -348,20 +432,26 @@
 
         acc = lax.fori_loop(0, inner // group, rows, acc)
         end = LAT_DEV - 1
-        return use(end, stencil(end, field[end - 1], down[...] * bottom_keep), acc)
-
-    def keep_columns(k, i, row):
-        rc_ref[k, 0, pl.ds(i, 1), :] = row[0:1]
-        rc_ref[k, 1, pl.ds(i, 1), :] = row[LON_DEV - 1 : LON_DEV]
-
-    def forward_state(field, k, old):
+        return use(end, stencil(end, field[end - 1], down), acc)
+
+    def first_sweep(k, use):
+        return fold(stage(
+            "sweep", sweep, g_ref.at[k], hv[k, 0, 1] * top_keep, hv[k, 1, 0] * bottom_keep,
+            hc.at[k, 0, 1], hc.at[k, 1, 0], use, zero,
+        ))
+
+    def second_sweep(k, field):
         def use(i, row, acc):
             high, low = halves(row)
             split_ref[i] = jnp.concatenate([high, low], axis=1)
             return acc
 
-        stage("sweep_u", sweep, field, k, use, 0)
-
+        rim(k)
+        stage(
+            "sweep_u", sweep, field, rim_rows[0], rim_rows[1], rim_cols.at[0], rim_cols.at[1], use, 0
+        )
+
+    def observe_state():
         def line_step(step, carry):
             for g in range(FORWARD_STEP):
                 base = pl.multiple_of((step * FORWARD_STEP + g) * LINES, LINES)
@@ -382,7 +472,7 @@
 
         stage("forward", lax.fori_loop, 0, groups // FORWARD_STEP, line_step, 0)
 
-    def forward_bias(i, beta):
+    def forward_bias(i):
         for b in range(blocks):
             for h in range(per):
                 j = b * per + h
@@ -406,11 +496,9 @@
                         total = jnp.where(which == b, mid[b * NPRED : (b + 1) * NPRED], total)
                     total = jnp.sum(total * preds_of(it, p), axis=0, keepdims=True)
                     looked += [total[:, :OBS_BLOCK], total[:, OBS_BLOCK:]]
-                f8 = y_ref[pl.ds(base, LINES), :] + jnp.concatenate(looked, axis=0)
-                if beta is not None:
-                    f8 = f8 + beta * f_ref[pl.ds(base, LINES), :]
+                f8 = kept_ref[i, pl.ds(base, LINES), :] + jnp.concatenate(looked, axis=0)
                 y8 = w_ref[pl.ds(base, LINES), :] * f8
-                f_ref[pl.ds(base, LINES), :] = f8
+                f_ref[i, pl.ds(base, LINES), :] = f8
                 y_ref[pl.ds(base, LINES), :] = y8
                 acc = acc + y8 * f8
             return acc
@@ -425,50 +513,58 @@
 
     part_ref[lines] = zero
     sums = adjoint_bias(1)
-    squares = across(0, squares)
-    stage("load_index", load_index.wait)
+    load_index.wait()
     stage("load_jac", load_jac.wait)
     halos = adjoint_state(0)
-    sums = across(1, sums)
+    squares = across(0, squares)
 
     def turn_step(it, carry):
         for l in range(LINES):
             turned_ref[it * LINES + l] = jnp.transpose(jac_of(it * LINES + l))
         return carry
 
-    stage("turn", lax.fori_loop, 0, groups, turn_step, 0)
+    turns = [groups * k // len(pieces) for k in range(len(pieces) + 1)]
+
+    def turn_some(k):
+        stage("turn", lax.fori_loop, turns[k], turns[k + 1], turn_step, 0)
+
+    sums = across(1, sums, turn_some)
     landed(halos)
 
     def use_first(i, row, acc):
         r0_ref[i] = row
-        keep_columns(0, i, row)
         return acc + row * row
 
-    pp_state = fold(stage("sweep", sweep, g_ref.at[0], 0, use_first, zero))
-    halos = halo(1, r0_ref, rc_ref.at[0])
+    pp_state = first_sweep(0, use_first)
     crossing = lon_tile(0, pp_state)
-    landed(owners)
+    second_sweep(0, r0_ref)
     for j in range(chunk):
-        spot = jnp.minimum(me * chunk + j, width - 1)
-        bp_c[j] = own_all[spot // own, lax.rem(spot, own)]
-    diag_c[...] = bp_c[...] + chunk_sum(0, squares)
-    r_c[...] = chunk_sum(1, sums)
-    p_c[...] = r_c[...] / diag_c[...]
-    gathers = gather(0, p_c[...])
-    around = lat_tile(0, rows_tile(lon_total(0, crossing), *dots((r_c, p_c), (r_c, r_c))))
-    landed(halos)
-    forward_state(r0_ref, 1, None)
+        @pl.when(spots[j] // own != z)
+        def _():
+            bias_copy(j, 1).wait_recv()
+
+    gathers = []
+    for k, part in enumerate(pieces):
+        diag_c[part] = bp_c[part] + chunk_sum(0, k, squares)
+        r_c[part] = chunk_sum(1, k, sums)
+        z_c[part] = r_c[part] / diag_c[part]
+        p_c[part] = z_c[part]
+        gathers += gather(0, k, z_c[part])
+    observe_state()
+    kept_ref[0] = y_ref[...]
+    opening = lat_tile(0, rows_tile(lon_total(0, crossing), *dots((r_c, p_c), (r_c, r_c))))
     landed(gathers)
-    totals = lat_total(0, around)
-    rz = spread(totals[0:1] + totals[1:2])
-    norms = [spread(totals[0:1] + totals[2:3])]
+    alphas, norms = [], []
     beta = None
-    alphas = []
     for turn in range(ITERS):
-        final = turn == ITERS - 1
-        observed = forward_bias(turn, None if beta is None else beta[0:1])
-        sums = adjoint_bias(2 + turn)
-        if turn > 0:
+        first, final = turn == 0, turn == ITERS - 1
+        event = 1 + 2 * turn
+        observed = forward_bias(turn)
+        totals = lat_total(event - 1, opening)
+        new = spread(totals[0:1] + totals[1:2])
+        norms.append(spread(totals[0:1] + totals[2:3]))
+        if not first:
+            beta = new / rz
             slope = beta[0:1]
 
             def p_step(it, acc):
@@ -480,64 +576,73 @@
                 return acc
 
             pp_state = fold(stage("p_step", lax.fori_loop, 0, LAT_DEV // 4, p_step, zero))
-            p_c[...] = tf[turn, me] + beta * p_c[...]
-        crossing = lon_tile(1 + 2 * turn, pp_state + observed)
+            joined = f_ref[turn] + slope * f_ref[turn - 1]
+            observed = fold(w_ref[...] * joined * joined)
+            p_c[...] = z_c[...] + beta * p_c[...]
+        rz = new
+        crossing = lon_tile(event, pp_state + observed)
+        sums = adjoint_bias(2 + turn)
+        pp_bias = total_of([bp_c[j] * p_c[j] * p_c[j] for j in range(chunk)])
+        around = lat_tile(event, rows_tile(lon_total(event, crossing), pp_bias))
         halos = adjoint_state(1 + turn)
-        pp_bias = total_of([bp_c[j] * p_c[j] * p_c[j] for j in range(chunk)])
-        around = lat_tile(1 + 2 * turn, rows_tile(lon_total(1 + 2 * turn, crossing), pp_bias))
         sums = across(2 + turn, sums)
-        totals = lat_total(1 + 2 * turn, around)
+        totals = lat_total(event, around)
         alpha = rz / spread(totals[0:1] + totals[1:2])
         alphas.append(alpha)
         line = alpha[0:1]
         landed(halos)
-        p_ref, old_ref = (p1_ref, r1_ref) if turn > 0 else (r0_ref, r0_ref)
+        old_ref = r0_ref if first else r1_ref
 
         def use_next(i, row, acc):
-            new = old_ref[i] - line * (p_ref[i] + row)
+            image = old_ref[i] + row
+            if first:
+                q_ref[i] = image
+                s_ref[i] = row
+            else:
+                image = image + slope * q_ref[i]
+            residual = old_ref[i] - line * image
             if not final:
-                r1_ref[i] = new
-                keep_columns(1, i, new)
-            return acc + new * new
-
-        rr_state = fold(stage("sweep", sweep, g_ref.at[1 + turn], 2 + 2 * turn, use_next, zero))
-        crossing = lon_tile(2 + 2 * turn, rr_state)
+                r1_ref[i] = residual
+            return acc + residual * residual
+
+        crossing = lon_tile(event + 1, first_sweep(1 + turn, use_next))
+        gathers = []
+        for k, part in enumerate(pieces):
+            image = bp_c[part] * z_c[part] + chunk_sum(2 + turn, k, sums)
+            if not first:
+                image = image + beta * q_c[part]
+            q_c[part] = image
+            r_c[part] = r_c[part] - alpha * image
+            z_c[part] = r_c[part] / diag_c[part]
+            if not final:
+                gathers += gather(turn + 1, k, z_c[part])
         if not final:
-            halos = halo(3 + 2 * turn, r1_ref, rc_ref.at[1])
-        image = bp_c[...] * p_c[...] + chunk_sum(2 + turn, sums)
-        r_c[...] = r_c[...] - alpha * image
-        z_c = r_c[...] / diag_c[...]
-        if not final:
-            gathers = gather(turn + 1, z_c)
-        around = lat_tile(
-            2 + 2 * turn, rows_tile(lon_total(2 + 2 * turn, crossing), *dots((r_c, z_c), (r_c, r_c)))
+            second_sweep(1 + turn, s_ref)
+            observe_state()
+            kept_ref[1] = kept_ref[0] - alpha[0:1] * (kept_ref[0] + y_ref[...])
+        opening = lat_tile(
+            event + 1, rows_tile(lon_total(event + 1, crossing), *dots((r_c, z_c), (r_c, r_c)))
         )
         if not final:
-            landed(halos)
-            forward_state(r1_ref, 3 + 2 * turn, None)
             landed(gathers)
-        else:
-            first_line, last_line = alphas[0][0:1], alphas[1][0:1]
-
-            def x_step(it, carry):
-                for k in range(4):
-                    i = it * 4 + k
-                    x_out[i] = first_line * r0_ref[i] + last_line * p1_ref[i]
-                return carry
-
-            stage("x_step", lax.fori_loop, 0, LAT_DEV // 4, x_step, 0)
-            for j in range(own):
-                spot = z * own + j
-                row, col = spot // chunk, lax.rem(spot, chunk)
-                start = tf[0, row, col]
-                bias_out[:, j * LANES : (j + 1) * LANES] = alphas[0] * start + alphas[1] * (
-                    tf[1, row, col] + beta * start
-                )
-        totals = lat_total(2 + 2 * turn, around)
-        new = spread(totals[0:1] + totals[1:2])
-        norms.append(spread(totals[0:1] + totals[2:3]))
-        beta = new / rz
-        rz = new
+    first_line, last_line = alphas[0][0:1], alphas[1][0:1]
+
+    def x_step(it, carry):
+        for k in range(4):
+            i = it * 4 + k
+            x_out[i] = first_line * r0_ref[i] + last_line * p1_ref[i]
+        return carry
+
+    stage("x_step", lax.fori_loop, 0, LAT_DEV // 4, x_step, 0)
+    for j in range(own):
+        spot = z * own + j
+        row, col = spot // chunk, lax.rem(spot, chunk)
+        start = tf[0, row, col]
+        bias_out[:, j * LANES : (j + 1) * LANES] = alphas[0] * start + alphas[1] * (
+            tf[1, row, col] + beta * start
+        )
+    totals = lat_total(2 * ITERS, opening)
+    norms.append(spread(totals[0:1] + totals[2:3]))
     lane = lax.broadcasted_iota(jnp.int32, TILE, 1)
     squares = jnp.zeros(TILE, F32)
     for j in range(ITERS + 1):
@@ -545,6 +650,14 @@
     norms_out[...] = jnp.sqrt(squares)
     for copy in pending:
         copy.wait_send()
+    for j in range(chunk):
+        @pl.when(spots[j] // own == z)
+        def _():
+            sources = own_ref.at[pl.ds(0, m - 1)]
+            pltpu.make_async_remote_copy(
+                src_ref=sources, dst_ref=sources, send_sem=o_s.at[j], recv_sem=o_r.at[j],
+                device_id=to_lon(1), device_id_type=pl.DeviceIdType.MESH,
+            ).wait_send()
 
 
 def publish(x_ref, bias_ref, norms_ref, x_out, bias_out, norms_out, row_ref, sems):
@@ -583,6 +696,7 @@
     slots = obs_precision.shape[0]
     lines = slots // OBS_BLOCK
     chunk = -(-width // n)
+    parts = min(PIECES, chunk)
     half = NPRED * blocks
     grid_lines = lambda a: a.reshape(lines, OBS_BLOCK)
     held = lambda a: pltpu.with_memory_space_constraint(a, pltpu.HBM)
@@ -590,27 +704,29 @@
     vb = lambda *s: pltpu.VMEM(s, BF16)
     vi = lambda *s: pltpu.VMEM(s, jnp.int32)
     sem = lambda *s: pltpu.SemaphoreType.DMA(s)
-    halos = 1 + 2 * ITERS
+    halos = 1 + ITERS
     tables = 2 + ITERS
     events = 1 + 2 * ITERS
     scratch = [
         vi(lines, OBS_BLOCK), vi(lines, OBS_BLOCK), vm(lines, OBS_BLOCK), vm(lines, OBS_BLOCK),
         vm(NPRED, slots), vb(slots, LEV),
         vb(lines, LEV, OBS_BLOCK), vb(lines // 2, CH_BLOCK, PAIR), vb(lines // 2, half, PAIR),
-        vm(lines, OBS_BLOCK), vm(lines, OBS_BLOCK), vm(lines, OBS_BLOCK), vm(lines + 1, LON_DEV, LEV),
+        vm(lines, OBS_BLOCK), vm(lines, OBS_BLOCK), vm(ITERS, lines, OBS_BLOCK), vm(lines + 1, LON_DEV, LEV),
         vi(8, LANES), pltpu.SMEM((8, LANES), jnp.int32),
-        vm(1 + ITERS, LAT_DEV, LON_DEV, LEV), vm(1 + ITERS, 2, LAT_DEV, LEV),
+        vm(1 + ITERS, LAT_DEV, LON_DEV, LEV), vm(1 + ITERS, 2, 2, LAT_DEV, LEV),
         vm(LAT_DEV, LON_DEV, LEV), vm(LAT_DEV, LON_DEV, LEV), vm(LAT_DEV, LON_DEV, LEV),
-        vm(2, 2, LAT_DEV, LEV), vb(LAT_DEV, LON_DEV, 2 * LEV),
+        vm(LAT_DEV, LON_DEV, LEV), vm(LAT_DEV, LON_DEV, LEV),
+        vm(ITERS, lines, OBS_BLOCK), vb(LAT_DEV, LON_DEV, 2 * LEV),
         vm(2 * half, CH_BLOCK), vm(tables, n, chunk, NPRED, LANES), vb(half, 2 * CH_BLOCK),
         vm(chunk, NPRED, LANES), vm(chunk, NPRED, LANES), vm(chunk, NPRED, LANES),
-        vm(chunk, NPRED, LANES), vm(m, own, NPRED, LANES),
-        vm(halos, LON_DEV, LEV), vm(halos, LON_DEV, LEV), vm(halos, 2, LAT_DEV, LEV),
+        vm(chunk, NPRED, LANES), vm(chunk, NPRED, LANES), vm(chunk, NPRED, LANES), vm(own, NPRED, LANES),
+        vm(halos, 2, 2, LON_DEV, LEV), vm(halos, 2, 2, LAT_DEV, LEV),
+        vm(halos, 4, 8, LEV), vm(2, LON_DEV, LEV), vm(2, LAT_DEV, LEV),
         vm(tables, n, chunk, NPRED, LANES), vm(tables, m, chunk, NPRED, LANES),
         vm(ITERS, n, chunk, NPRED, LANES), vm(events, m, 8, LANES), vm(events, n, 8, LANES),
-        sem(6), sem(1), sem(m), sem(m), sem(halos, 4), sem(halos, 4), sem(tables, n), sem(tables, n),
-        sem(tables, m), sem(tables, m), sem(ITERS, n), sem(ITERS, n), sem(events, m), sem(events, m),
-        sem(events, n), sem(events, n),
+        sem(6), sem(1), sem(chunk), sem(chunk), sem(halos, 3), sem(halos, 3),
+        sem(tables, parts), sem(tables, parts), sem(tables, parts), sem(tables, parts),
+        sem(ITERS, parts), sem(ITERS, parts), sem(events), sem(events), sem(events), sem(events),
     ]
     VM = pl.BlockSpec(memory_space=pltpu.VMEM)
     HB = pl.BlockSpec(memory_space=pltpu.HBM)

time: 75.3 us -> 68 us (0.903)
  Pallas kernels: 73.9 us -> 66.5 us
    pallas_call x1, Pallas kernels: 72.9 us -> 65.5 us  [body(): pl.pallas_call(functools.partial(kernel, n, m, own, blocks, lines, chunk)...]
where the time goes in v3:
time: 68 us; the launch traced here: 67.8 us
  Pallas kernels  66.5 us (98%)
  between operations  1.29 us (2%)
    pallas_call x1, Pallas kernels, body(): pl.pallas_call(functools.partial(kernel, n, m, own, blocks, lines, chunk)...  65.5 us

profile of v3, /device:TPU:0, one launch (start us, length us, event | category | flops | bytes accessed | tf_op | source)
XLA Modules:
  0.0 67.8 jit_solution(3834900519610922783)
XLA Ops:
  1.3 65.5 %cg.1 = (f32[32,64,128]{2,1,0:T(8,128)S(1)}, f32[8,1280]{1,0:T(8,128)S(1)}, f32[8,128]{1,0:T(8,128)S(1)}) custom-call(s32[1,1]{1,0:T(1,128)S(6)} %copy.12.refs_0_, f32[1,128]{1,0:T(1,128)} %bitcast.9, f32[8,1280]{1,0:T(8,128)} %refs_2_.1, s32[128,128]{1,0:T(8,128)} %bitcast.5, s32[128,128]{1,0:T(8,128)} %bitcast.6, f32[128,128]{1,0:T(8,128)} %bitcast.7, ...), custom_call_target="tpu_custom_call" | custom-call | tf_op jit(solution)/shard_map/cg/pallas_call | solution.py:733
  66.8 1.0 %publish.1 = (f32[32,64,128]{2,1,0:T(8,128)}, f32[8,1280]{1,0:T(8,128)}, f32[3]{0:T(128)}) custom-call(f32[32,64,128]{2,1,0:T(8,128)S(1)} %get-tuple-element.6.x_ref, f32[8,1280]{1,0:T(8,128)S(1)} %get-tuple-element.7.bias_ref, f32[8,128]{1,0:T(8,128)S(1)} %get-tuple-element.8.norms_ref), custom_call_target="tpu_custom_call" | custom-call | tf_op jit(solution)/shard_map/publish/pallas_call | solution.py:749

commit v4 on v3

--- a/solution.py
+++ b/solution.py
@@ -19,7 +19,7 @@
 SQUARE_STEP, TABLE_STEP, LOOK_STEP, ADJOINT_STEP, FORWARD_STEP = 4, 8, 8, 4, 4
 PAIR = 2 * OBS_BLOCK
 LANES = 128
-PIECES = 2
+PIECES = 1
 TILE = (8, LANES)
 F32 = jnp.float32
 BF16 = jnp.bfloat16
@@ -107,17 +107,6 @@
         return {"swath": lax.rem(me + d, n), "chan": lax.rem(z + e, m)}
 
     corners = [(1, 1), (1, m - 1), (n - 1, 1), (n - 1, m - 1)]
-    barrier = pltpu.get_barrier_semaphore()
-    for d in range(1, n):
-        pl.semaphore_signal(barrier, inc=1, device_id=to_lat(d), device_id_type=pl.DeviceIdType.MESH)
-    for d in range(1, m):
-        pl.semaphore_signal(barrier, inc=1, device_id=to_lon(d), device_id_type=pl.DeviceIdType.MESH)
-
-    for d, e in corners:
-        pl.semaphore_signal(
-            barrier, inc=1, device_id=diagonal(d, e), device_id_type=pl.DeviceIdType.MESH
-        )
-
     loads = []
     for k, (src, dst) in enumerate((
         (chan_h, chan_ref), (prec_h, prec_ref), (pred_h, pred_ref),
@@ -126,6 +115,17 @@
         copy = pltpu.make_async_copy(src, dst, in_s.at[k])
         copy.start()
         loads.append(copy)
+    barrier = pltpu.get_barrier_semaphore()
+    for d in range(1, n):
+        pl.semaphore_signal(barrier, inc=1, device_id=to_lat(d), device_id_type=pl.DeviceIdType.MESH)
+    for d in range(1, m):
+        pl.semaphore_signal(barrier, inc=1, device_id=to_lon(d), device_id_type=pl.DeviceIdType.MESH)
+
+    for d, e in corners:
+        pl.semaphore_signal(
+            barrier, inc=1, device_id=diagonal(d, e), device_id_type=pl.DeviceIdType.MESH
+        )
+
     load_chan, load_prec, load_pred, load_innov, load_cell, load_jac = loads
 
     count = count_ref[0, 0]
@@ -641,15 +641,8 @@
         bias_out[:, j * LANES : (j + 1) * LANES] = alphas[0] * start + alphas[1] * (
             tf[1, row, col] + beta * start
         )
-    totals = lat_total(2 * ITERS, opening)
-    norms.append(spread(totals[0:1] + totals[2:3]))
-    lane = lax.broadcasted_iota(jnp.int32, TILE, 1)
-    squares = jnp.zeros(TILE, F32)
-    for j in range(ITERS + 1):
-        squares = jnp.where(lane == j, norms[j], squares)
-    norms_out[...] = jnp.sqrt(squares)
-    for copy in pending:
-        copy.wait_send()
+    while len(pending) > 1:
+        pending.pop(0).wait_send()
     for j in range(chunk):
         @pl.when(spots[j] // own == z)
         def _():
@@ -658,6 +651,14 @@
                 src_ref=sources, dst_ref=sources, send_sem=o_s.at[j], recv_sem=o_r.at[j],
                 device_id=to_lon(1), device_id_type=pl.DeviceIdType.MESH,
             ).wait_send()
+    totals = lat_total(2 * ITERS, opening)
+    norms.append(spread(totals[0:1] + totals[2:3]))
+    lane = lax.broadcasted_iota(jnp.int32, TILE, 1)
+    squares = jnp.zeros(TILE, F32)
+    for j in range(ITERS + 1):
+        squares = jnp.where(lane == j, norms[j], squares)
+    norms_out[...] = jnp.sqrt(squares)
+    pending.pop().wait_send()
 
 
 def publish(x_ref, bias_ref, norms_ref, x_out, bias_out, norms_out, row_ref, sems):

time: 68 us -> 67.6 us (level)
  no operation moved by 1% of the time
where the time goes in v4:
time: 67.6 us; the launch traced here: 67.4 us
  Pallas kernels  66.1 us (98%)
  between operations  1.29 us (2%)
    pallas_call x1, Pallas kernels, body(): pl.pallas_call(functools.partial(kernel, n, m, own, blocks, lines, chunk)...  65.1 us

profile of v4, /device:TPU:0, one launch (start us, length us, event | category | flops | bytes accessed | tf_op | source)
XLA Modules:
  0.0 67.4 jit_solution(3033877746884341268)
XLA Ops:
  1.3 65.1 %cg.1 = (f32[32,64,128]{2,1,0:T(8,128)S(1)}, f32[8,1280]{1,0:T(8,128)S(1)}, f32[8,128]{1,0:T(8,128)S(1)}) custom-call(s32[1,1]{1,0:T(1,128)S(6)} %copy.12.refs_0_, f32[1,128]{1,0:T(1,128)} %bitcast.9, f32[8,1280]{1,0:T(8,128)} %refs_2_.1, s32[128,128]{1,0:T(8,128)} %bitcast.5, s32[128,128]{1,0:T(8,128)} %bitcast.6, f32[128,128]{1,0:T(8,128)} %bitcast.7, ...), custom_call_target="tpu_custom_call" | custom-call | tf_op jit(solution)/shard_map/cg/pallas_call | solution.py:734
  66.4 1.0 %publish.1 = (f32[32,64,128]{2,1,0:T(8,128)}, f32[8,1280]{1,0:T(8,128)}, f32[3]{0:T(128)}) custom-call(f32[32,64,128]{2,1,0:T(8,128)S(1)} %get-tuple-element.6.x_ref, f32[8,1280]{1,0:T(8,128)S(1)} %get-tuple-element.7.bias_ref, f32[8,128]{1,0:T(8,128)S(1)} %get-tuple-element.8.norms_ref), custom_call_target="tpu_custom_call" | custom-call | tf_op jit(solution)/shard_map/publish/pallas_call | solution.py:750
